TPU v7x, 256 devices: a whole 4x4x8 slice. The times are simulated.
256 devices in a mesh: section: 2 (over core), tile: 128 (over y, z, x).
Axes of the slice: x: 4, y: 4, z: 8, core: 2. Of those that a mesh axis runs over, the one named last changes fastest.
Arguments:
- object_slices: float32 [2, 4096, 2, 16, 128], P('section', 'tile'), may hold values from -4 to 4
- probe_wave: float32 [2, 256, 256], replicated, may hold values from -4 to 4
- intensities: float32 [256, 256, 256], P('tile'), may hold values from 0 to 2
- send_list: int32 [128, 2, 128, 2], P('tile'), may hold values from -1 to 31, as said below
- cell_slot: int32 [256, 32], P('tile'), may hold values from 0 to 255, as said below
Outputs:
- object_gradient: float32 [2, 4096, 2, 16, 128], P('section', 'tile')
Inputs may be any that keep to these rules, and one draw needn't show every extreme that they name: `cell_slot`: the cells of one device's batch name distinct slots; the slots named by a batch are exactly the entries of send_list for that device and batch that are not -1. `send_list`: entry [o, m, d, c] is a patch index of owner o exactly when slot o * 2 + c is named by a cell of device d in batch m, and -1 otherwise. In every batch of every device, some owner has all 2 of its places used.
All inputs are finite; a program needn't handle non-finite values.
Results may differ from a plain program's by a relative error of at most 0.0003.
Values sent between devices are 32-bit elements; how exact they have to be, the bound alone decides.
A program may use at most 64 MiB of HBM per device.

v0:
```python
import functools
import math

import jax
import jax.numpy as jnp
from jax import lax
from jax.sharding import PartitionSpec as P

W = 256
PW = 128
PR = 16
MB = 2
POS_MB = 1
CELLS = 32


PHASE_SCALE = 20.0


def swapped(block, axis, bit):
    count = lax.axis_size(axis)
    route = []
    for low in range(count):
        high = low | 1 << bit
        if high != low and high < count:
            route += [(low, high), (high, low)]
    return lax.ppermute(block, axis, route)


def stitch(cell_patches):
    row_count = cell_patches.shape[0]
    arranged = cell_patches.reshape(row_count, W // PR, W // PW, 2, PR, PW)
    return jnp.transpose(arranged, (3, 0, 1, 4, 2, 5)).reshape(2, row_count, W, W)


def unstitch(wavefield):
    row_count = wavefield.shape[1]
    arranged = wavefield.reshape(2, row_count, W // PR, PR, W // PW, PW)
    return jnp.transpose(arranged, (1, 2, 4, 0, 3, 5)).reshape(row_count, CELLS, 2, PR, PW)


def dft_tables():
    indices = jnp.arange(W, dtype=jnp.int32)
    product = indices[:, None] * indices[None, :] % W
    angles = 2.0 * math.pi / W * product.astype(jnp.float32)
    scaling = 1.0 / math.sqrt(W)
    return (jnp.cos(angles) * scaling, jnp.sin(angles) * scaling)


def filter_table():
    indices = jnp.arange(W, dtype=jnp.int32)
    frequency = jnp.where(indices < W // 2, indices, indices - W)
    squared = frequency[:, None] * frequency[:, None] + frequency[None, :] * frequency[None, :]
    phases = PHASE_SCALE * squared.astype(jnp.float32) / (W * W)
    return jnp.stack([jnp.cos(phases), -jnp.sin(phases)])


def complex_times(factor, second_factor):
    return jnp.stack(
        [
            factor[0] * second_factor[0] - factor[1] * second_factor[1],
            factor[0] * second_factor[1] + factor[1] * second_factor[0],
        ]
    )


def conjugate(complex_value):
    return jnp.stack([complex_value[0], -complex_value[1]])


def transform(wavefield, tables, inverse):
    cos_table, sin_table = tables
    signed = sin_table if inverse else -sin_table
    highest = lax.Precision.HIGHEST
    cosine_part = jnp.einsum("ij,cpjk->cpik", cos_table, wavefield, precision=highest)
    sine_part = jnp.einsum("ij,cpjk->cpik", signed, wavefield, precision=highest)
    middle = jnp.stack([cosine_part[0] - sine_part[1], cosine_part[1] + sine_part[0]])
    cosine_part = jnp.einsum("cpij,jk->cpik", middle, cos_table, precision=highest)
    sine_part = jnp.einsum("cpij,jk->cpik", middle, signed, precision=highest)
    return jnp.stack([cosine_part[0] - sine_part[1], cosine_part[1] + sine_part[0]])


def forward_first(window_field, probe_wave, tables, transfer):
    entering = complex_times(probe_wave[:, None], window_field)
    spectrum = complex_times(transfer[:, None], transform(entering, tables, False))
    return transform(spectrum, tables, True)


def last_pass(window_field, propagated, measured, tables):
    far_field = transform(complex_times(propagated, window_field), tables, False)
    misfit = (far_field[0] * far_field[0] + far_field[1] * far_field[1] - measured)[
        None
    ] * far_field
    back_far = transform(misfit, tables, True)
    return (
        complex_times(conjugate(window_field), back_far),
        complex_times(conjugate(propagated), back_far),
    )


def adjoint_first(arriving, probe_wave, tables, transfer):
    spectrum = complex_times(conjugate(transfer)[:, None], transform(arriving, tables, False))
    return complex_times(conjugate(probe_wave)[:, None], transform(spectrum, tables, True))


def front_tick(
    tick_index, batch_count, windows, incoming, probe_wave, tables, transfer, empty_wave
):
    if tick_index < batch_count:
        outgoing = forward_first(windows[tick_index], probe_wave, tables, transfer)
    else:
        outgoing = empty_wave
    if tick_index >= 2:
        gradient = adjoint_first(incoming, probe_wave, tables, transfer)
    else:
        gradient = empty_wave
    return (outgoing, gradient)


def back_tick(tick_index, batch_count, windows, incoming, measured_list, tables, empty_wave):
    if 1 <= tick_index <= batch_count:
        return last_pass(windows[tick_index - 1], incoming, measured_list[tick_index - 1], tables)
    return (empty_wave, empty_wave)


def roster(windows, measured_list, probe_wave, leading, tables, transfer, pass_wave):
    batch_count = len(windows)
    empty_wave = jnp.zeros_like(windows[0])
    incoming = empty_wave
    results = []
    for tick_index in range(batch_count + 2):
        front_work = functools.partial(
            front_tick,
            tick_index,
            batch_count,
            windows,
            incoming,
            probe_wave,
            tables,
            transfer,
            empty_wave,
        )
        back_work = functools.partial(
            back_tick, tick_index, batch_count, windows, incoming, measured_list, tables, empty_wave
        )
        outgoing, gradient = lax.cond(leading, front_work, back_work)
        results.append(gradient)
        if tick_index <= batch_count:
            incoming = pass_wave(outgoing)
    return [jnp.where(leading, results[2], results[1])]


def pick_patches(owned_blocks, indices):
    clamped = jnp.maximum(indices, 0)
    present = (indices >= 0).astype(jnp.float32)
    return owned_blocks[clamped] * present[..., None, None, None]


def slot_table(arrived, slot_ids):
    flattened = arrived.reshape((-1,) + arrived.shape[-3:])
    return stitch(flattened[slot_ids])


def slot_sums(gradient, slot_ids, slot_count):
    cell_patches = unstitch(gradient)
    flattened = cell_patches.reshape((-1,) + cell_patches.shape[2:])
    return jax.ops.segment_sum(flattened, slot_ids.reshape(-1), num_segments=slot_count)


def accumulate(returned, indices, block_count):
    target = jnp.where(indices < 0, block_count, indices).reshape(-1)
    flattened = returned.reshape((-1,) + returned.shape[-3:])
    block_sums = jax.ops.segment_sum(flattened, target, num_segments=block_count + 1)
    return block_sums[:block_count]


def batch_rows(values, batch_index):
    return values[batch_index * POS_MB : (batch_index + 1) * POS_MB]


def body(object_slices, probe_wave, intensities, send_list, cell_slot):
    leading = lax.axis_index("section") == 0
    tile_count = lax.axis_size("tile")
    capacity = send_list.shape[3]
    owned_blocks = object_slices[0]
    block_count = owned_blocks.shape[0]
    send_plan = send_list[0]
    tables = dft_tables()
    transfer = filter_table()
    slot_count = tile_count * capacity
    outbound = jnp.swapaxes(send_plan, 0, 1)
    arrived = lax.all_to_all(
        pick_patches(owned_blocks, outbound), "tile", split_axis=0, concat_axis=0, tiled=True
    )
    pieces = [
        slot_table(arrived[:, batch_index], batch_rows(cell_slot, batch_index))
        for batch_index in range(MB)
    ]
    windows = [jnp.concatenate(pieces, axis=1)]

    def pass_whole(outgoing):
        return swapped(outgoing, "section", 0)

    gradients = roster(windows, [intensities], probe_wave, leading, tables, transfer, pass_whole)
    slot_grads = jnp.stack(
        [
            slot_sums(
                gradients[0][:, batch_index * POS_MB : (batch_index + 1) * POS_MB],
                batch_rows(cell_slot, batch_index),
                slot_count,
            ).reshape(tile_count, capacity, 2, PR, PW)
            for batch_index in range(MB)
        ],
        axis=1,
    )
    returned = lax.all_to_all(slot_grads, "tile", split_axis=0, concat_axis=0, tiled=True)
    gradient_sum = accumulate(returned, outbound, block_count)
    return gradient_sum[None]


def solution(mesh):
    in_specs = (
        P("section", "tile", None, None, None),
        P(),
        P("tile", None, None),
        P("tile", None, None, None),
        P("tile", None),
    )
    out_specs = P("section", "tile", None, None, None)
    return jax.shard_map(body, mesh=mesh, in_specs=in_specs, out_specs=out_specs, check_vma=False)
```

profile of v0, /device:TPU:32, one launch (start us, length us, event | category | flops | bytes accessed | tf_op | source)
XLA Modules:
  0.0 555.3 jit_solution(13777035243714689943)
XLA Ops:
  2.0 4.4 gather_fusion
  6.4 5.8 %broadcast_multiply_fusion = f32[128,2,2,2,16,128]{5,4,3,2,1,0:T(8,128)} fusion(f32[128,2,2,2,16,128]{5,4,3,2,1,0:T(8,128)} %bitcast.202, f32[128,2,2]{2,1,0:T(2,128)S(1)} %copy.89), kind=kLoop, calls=%fused_computation.147 | loop fusion | flops 2097152 | bytes 16779264 | tf_op jit(solution)/shard_map/mul | solution.py:156
  12.3 15.6 %all-to-all-start = ((f32[128,2,2,2,16,128]{5,4,3,2,1,0:T(8,128)}), f32[128,2,2,2,16,128]{5,4,3,2,1,0:T(8,128)}, u32[]{:S(2)}, u32[]{:S(2)}) async-start(f32[128,2,2,2,16,128]{5,4,3,2,1,0:T(8,128)} %broadcast_multiply_fusion), calls=%async_computation | async-start | bytes 16777216 | tf_op jit(solution)/shard_map/all_to_all | solution.py:192
  30.8 183.3 %all-to-all-done = f32[128,2,2,2,16,128]{5,4,3,2,1,0:T(8,128)} async-done(((f32[128,2,2,2,16,128]{5,4,3,2,1,0:T(8,128)}), f32[128,2,2,2,16,128]{5,4,3,2,1,0:T(8,128)}, u32[]{:S(2)}, u32[]{:S(2)}) %all-to-all-start) | async-done | bytes 8388640 | tf_op jit(solution)/shard_map/all_to_all | solution.py:192
  214.2 8.7 %fusion.76 = (f32[128,1,2,2,16,128]{5,4,3,2,1,0:T(8,128)}, f32[128,1,2,2,16,128]{5,4,3,2,1,0:T(8,128)}) fusion(f32[128,2,2,2,16,128]{5,4,3,2,1,0:T(8,128)} %all-to-all-done), kind=kLoop, calls=%fused_computation.181 | loop fusion | bytes 16777216 | tf_op jit(solution)/shard_map/slice | solution.py:196
  222.8 2.8 gather_fusion.1
  226.0 2.8 gather_fusion.2
  230.2 26.8 %conditional.3 = (f32[2,2,256,256]{3,2,1,0:T(8,128)S(1)}) conditional(s32[]{:T(128)} %convert_element_type.81, () %tuple.26, (f32[2,256,256]{2,1,0:T(8,128)}, f32[2,256,256]{2,1,0:T(8,128)S(1)}, f32[2,2,256,256]{3,1,2,0:T(2,128)S(1)}, f32[256,256]{1,0:T(8,128)S(1)}, f32[256,256]{1,0:T(8,128)S(1)}, /*index=5*/f32[256,256]{1,0:T(8,128)S(1)}, ...), branch_computations={%region_0.1_spmd, %region_1.2_spmd} | conditional | flops 6447562752 | bytes 44040228 | solution.py:146
  235.4 1.8 fusion.3
  237.2 1.8 fusion.2
  239.2 1.8 convolution_bitcast_fusion.1
  241.1 1.8 convolution_bitcast_fusion
  258.3 2.9 collective-permute-done
  261.1 2.1 conditional.4
  263.3 15.3 %collective-permute-start.1 = (f32[2,2,256,256]{2,3,1,0:T(8,128)}, f32[2,2,256,256]{2,3,1,0:T(8,128)S(1)}, u32[]{:S(2)}, u32[]{:S(2)}) collective-permute-start(f32[2,2,256,256]{2,3,1,0:T(8,128)} %get-tuple-element.106), channel_id=1, source_target_pairs={{0,128},{128,0},{1,129},{129,1},{2,130},{130,2},{3,131},{131,3},{4... | collective-permute-start | bytes 3145736 | tf_op jit(solution)/shard_map/ppermute | solution.py:27
  278.6 2.4 collective-permute-done.1
  281.0 16.2 %conditional.5 = (f32[2,2,256,256]{3,2,1,0:T(8,128)S(1)}) conditional(s32[]{:T(128)} %convert_element_type.81, () %tuple.25, (f32[2,256,256]{2,1,0:T(8,128)}, f32[1,256,256]{2,1,0:T(8,128)S(1)}, f32[1,256,256]{2,1,0:T(8,128)S(1)}, f32[2,2,256,256]{2,3,1,0:T(8,128)S(1)}, f32[256,256]{1,0:T(8,128)S(1)}, /*index=5*/f32[256,256]{1,0:T(8,128)S(1)}, ...), branch_computations={%region_4.5_spmd, %region_5.6_spmd} | conditional | flops 6447235072 | bytes 39321636 | solution.py:146
  283.2 1.8 fusion.49
  285.0 1.8 fusion.48
  286.9 2.0 multiply_sine_fusion
  289.1 1.9 convolution_bitcast_fusion.9
  291.0 1.9 convolution_bitcast_fusion.8
  293.0 1.8 fusion.47
  294.8 1.8 fusion.46
  298.2 2.5 broadcast.143.clone.1
  300.6 4.3 scatter_fusion
  304.9 2.5 broadcast.143.clone
  307.5 4.3 scatter_fusion.1
  311.8 8.7 %pad_maximum_fusion.34 = f32[128,2,2,2,16,128]{5,4,3,2,1,0:T(8,128)} fusion(f32[128,1,2,2,16,128]{5,4,3,2,1,0:T(8,128)} %bitcast.204, f32[128,1,2,2,16,128]{5,4,3,2,1,0:T(8,128)} %bitcast.203), kind=kLoop, calls=%fused_computation.146 | loop fusion | flops 2097152 | bytes 16777216 | tf_op jit(solution)/shard_map/stack | solution.py:205
  320.4 8.6 %all-to-all-start.1 = ((f32[128,2,2,2,16,128]{5,4,3,2,1,0:T(8,128)}), f32[128,2,2,2,16,128]{5,4,3,2,1,0:T(8,128)}, u32[]{:S(2)}, u32[]{:S(2)}) async-start(f32[128,2,2,2,16,128]{5,4,3,2,1,0:T(8,128)} %pad_maximum_fusion.34), calls=%async_computation.1 | async-start | bytes 16777216 | tf_op jit(solution)/shard_map/all_to_all | solution.py:216
  329.4 179.2 %all-to-all-done.1 = f32[128,2,2,2,16,128]{5,4,3,2,1,0:T(8,128)} async-done(((f32[128,2,2,2,16,128]{5,4,3,2,1,0:T(8,128)}), f32[128,2,2,2,16,128]{5,4,3,2,1,0:T(8,128)}, u32[]{:S(2)}, u32[]{:S(2)}) %all-to-all-start.1) | async-done | bytes 8388640 | tf_op jit(solution)/shard_map/all_to_all | solution.py:216
  508.6 45.4 %scatter_fusion.2 = f32[33,2,16,128]{3,2,1,0:T(8,128)S(1)} fusion(f32[33,2,16,128]{3,2,1,0:T(8,128)S(1)} %broadcast_in_dim.27, s32[512]{0:T(512)S(1)} %reshape.212, f32[512,2,16,128]{3,2,1,0:T(8,128)} %bitcast.92), kind=kCustom, calls=%fused_computation.5 | custom fusion | flops 2097152 | bytes 25167872 | tf_op jit(solution)/shard_map/scatter-add | solution.py:173
  (64 shorter events, 23.4 us)
Async XLA Ops:
  0.0 2.0 copy-start
  12.2 15.6 %copy-start.8 = (s32[2,32]{1,0:T(2,128)S(1)}, s32[2,32]{1,0:T(2,128)}, u32[]{:S(2)}) copy-start(s32[2,32]{1,0:T(2,128)} %param.15) | copy-start | bytes 772
  12.3 201.9 %all-to-all-start = ((f32[128,2,2,2,16,128]{5,4,3,2,1,0:T(8,128)}), f32[128,2,2,2,16,128]{5,4,3,2,1,0:T(8,128)}, u32[]{:S(2)}, u32[]{:S(2)}) async-start(f32[128,2,2,2,16,128]{5,4,3,2,1,0:T(8,128)} %broadcast_multiply_fusion), calls=%async_computation | async-start | bytes 16777216 | tf_op jit(solution)/shard_map/all_to_all | solution.py:192
  30.8 199.3 %copy-start.4 = (f32[2,256,256]{2,1,0:T(8,128)S(1)}, f32[2,256,256]{2,1,0:T(8,128)}, u32[]{:S(2)}) copy-start(f32[2,256,256]{2,1,0:T(8,128)} %param.12) | copy-start | bytes 1572868
  231.2 7.8 %copy-start.6 = (f32[2,256,256]{2,1,0:T(8,128)S(1)}, f32[2,256,256]{2,1,0:T(8,128)}, u32[]{:S(2)}) copy-start(f32[2,256,256]{2,1,0:T(8,128)} %get-tuple-element.51) | copy-start | bytes 1572868 | tf_op jit(solution)/shard_map/cond
  258.3 2.9 collective-permute-start
  263.3 17.8 %collective-permute-start.1 = (f32[2,2,256,256]{2,3,1,0:T(8,128)}, f32[2,2,256,256]{2,3,1,0:T(8,128)S(1)}, u32[]{:S(2)}, u32[]{:S(2)}) collective-permute-start(f32[2,2,256,256]{2,3,1,0:T(8,128)} %get-tuple-element.106), channel_id=1, source_target_pairs={{0,128},{128,0},{1,129},{129,1},{2,130},{130,2},{3,131},{131,3},{4... | collective-permute-start | bytes 3145736 | tf_op jit(solution)/shard_map/ppermute | solution.py:27
  288.9 7.8 %copy-start.5 = (f32[2,256,256]{2,1,0:T(8,128)S(1)}, f32[2,256,256]{2,1,0:T(8,128)}, u32[]{:S(2)}) copy-start(f32[2,256,256]{2,1,0:T(8,128)} %get-tuple-element.90) | copy-start | bytes 1572868 | tf_op jit(solution)/shard_map/cond
  320.4 188.1 %all-to-all-start.1 = ((f32[128,2,2,2,16,128]{5,4,3,2,1,0:T(8,128)}), f32[128,2,2,2,16,128]{5,4,3,2,1,0:T(8,128)}, u32[]{:S(2)}, u32[]{:S(2)}) async-start(f32[128,2,2,2,16,128]{5,4,3,2,1,0:T(8,128)} %pad_maximum_fusion.34), calls=%async_computation.1 | async-start | bytes 16777216 | tf_op jit(solution)/shard_map/all_to_all | solution.py:216
  508.6 46.3 %copy-start.1 = (f32[1,32,2,16,128]{4,3,2,1,0:T(8,128)S(1)}, f32[1,32,2,16,128]{4,3,2,1,0:T(8,128)}, u32[]{:S(2)}) copy-start(f32[1,32,2,16,128]{4,3,2,1,0:T(8,128)} %param.11) | copy-start | bytes 1572868
where the time goes:
time: 564 us; the launch traced here: 555 us
  waiting for transfers between devices  368 us (65%)
  other arithmetic  78.6 us (14%)
  starting transfers between devices  39.4 us (7%)
  local copies, waits for them, and re-layouts  31.2 us (6%)
  matrix products  26 us (5%)
  loops' own time  11.5 us (2%)
    all_to_all x1, waiting for transfers between devices, body(): lax.all_to_all(pick_patches(owned_blocks, outbound), 'tile', split_axis=0...  183 us
    all_to_all x1, waiting for transfers between devices, body(): lax.all_to_all(slot_grads, 'tile', split_axis=0, concat_axis=0, tiled=True)  179 us
    scatter-add x1, other arithmetic, accumulate(): jax.ops.segment_sum(flattened, target, num_segments=block_count + 1)  45.4 us
    all_to_all x1, starting transfers between devices, body(): lax.all_to_all(pick_patches(owned_blocks, outbound), 'tile', split_axis=0...  15.6 us
    ppermute x2, starting transfers between devices, swapped(): return lax.ppermute(block, axis, route)  15.3 us
    another operation x3, loops' own time, roster(): outgoing, gradient = lax.cond(leading, front_work, back_work)  11.5 us
  transfers between devices with their start and end apart: 4, of which 4 were waited for; matrix products, arithmetic and copies ran while one was open for 1% of the time, Pallas kernels for 0%

commit v1 on v0

v1 whole, which is shorter than its diff:
```python
import functools

import jax
import jax.numpy as jnp
import ml_dtypes
import numpy as np
from jax import lax
from jax.experimental import pallas as pl
from jax.experimental.pallas import tpu as pltpu
from jax.sharding import PartitionSpec as P

W = 256
PW = 128
PR = 16
MB = 2
CELLS = 32
NX, NY, NZ = 4, 4, 8
PLANE = NX * NY
OWN = 32
COLUMN = NZ * OWN
PLACES = 14
ROWS = PLANE * PLACES
CHUNKS = 4
PHASE_SCALE = 20.0
MESH = pl.DeviceIdType.MESH
F32 = jnp.float32
I32 = jnp.int32
BF16 = jnp.bfloat16


def stacked_parts(matrix):
    rows = np.concatenate([matrix.real, matrix.imag], axis=0).astype(np.float32)
    high = rows.astype(ml_dtypes.bfloat16)
    low = (rows - high.astype(np.float32)).astype(ml_dtypes.bfloat16)
    return np.concatenate([high, high, low], axis=1)


def matrix_tables():
    index = np.arange(W)
    product = np.outer(index, index) % W
    dft = np.exp(-2j * np.pi * product / W) / np.sqrt(W)
    frequency = np.where(index < W // 2, index, index - W).astype(np.float64)
    diagonal = np.exp(-1j * PHASE_SCALE * frequency**2 / (W * W))
    move = np.conj(dft) @ (diagonal[:, None] * dft)
    move = (move + move.T) / 2
    return stacked_parts(dft), stacked_parts(move)


def place():
    tile = lax.axis_index("tile")
    core = lax.axis_index("section")
    y = tile // (NZ * NX)
    z = (tile // NX) % NZ
    x = tile % NX
    return core, y, z, x


def plane_tile(q, z):
    return (q // NX) * (NZ * NX) + z * NX + q % NX


def iota(shape, axis):
    return lax.broadcasted_iota(I32, shape, axis)


def to_column(row):
    n = row.shape[1]
    wide = jnp.broadcast_to(row, (n, n))
    return jnp.sum(jnp.where(iota((n, n), 0) == iota((n, n), 1), wide, 0.0), axis=1, keepdims=True)


def quotient(values, divisor, count):
    total = jnp.zeros(values.shape, I32)
    for step in range(1, count):
        total = total + jnp.where(values >= divisor * step, 1, 0)
    return total


def hops(chunk, direction):
    return 4 if (chunk % 2 == 0) == (direction > 0) else 3


def gather_kernel(
    obj,
    meta,
    cells,
    win,
    tab,
    flag,
    ag,
    metas,
    metain,
    tables,
    pick,
    slot,
    pack,
    recv,
    mark,
    marks,
    other,
    ag_send,
    ag_recv,
    meta_send,
    meta_recv,
    mark_send,
    mark_recv,
    xy_send,
    xy_recv,
    pair_send,
    pair_recv,
    local_sem,
):
    core, y, z, x = place()
    mine = y * NX + x
    barrier = pltpu.get_barrier_semaphore()

    def ring_device(zz):
        return (core, y * (NZ * NX) + zz * NX + x)

    def plane_device(q):
        return (core, plane_tile(q, z))

    def greet_ring(step, carry):
        pl.semaphore_signal(
            barrier, inc=1, device_id=ring_device((z + step) % NZ), device_id_type=MESH
        )
        return carry

    def greet_plane(step, carry):
        pl.semaphore_signal(
            barrier, inc=1, device_id=plane_device((mine + step) % PLANE), device_id_type=MESH
        )
        return carry

    partner = (1 - core, y * (NZ * NX) + z * NX + x)
    lax.fori_loop(1, NZ, greet_ring, 0)
    lax.fori_loop(1, PLANE, greet_plane, 0)
    pl.semaphore_signal(barrier, inc=1, device_id=partner, device_id_type=MESH)
    pl.semaphore_wait(barrier, NZ + PLANE - 1)

    def ring_copy(chunk, direction, hop):
        block = (z - direction * (hop - 1) + 2 * NZ) % NZ
        place_of = ag[chunk].at[pl.ds(block * OWN, OWN)]
        side = 0 if direction > 0 else 1
        return pltpu.make_async_remote_copy(
            src_ref=obj.at[:, chunk] if hop == 1 else place_of,
            dst_ref=place_of,
            send_sem=ag_send.at[chunk, side, hop - 1],
            recv_sem=ag_recv.at[chunk, side, hop - 1],
            device_id=ring_device((z + direction + NZ) % NZ),
            device_id_type=MESH,
        )

    def ring_arrival(chunk, direction, hop):
        block = (z - direction * hop + 2 * NZ) % NZ
        place_of = ag[chunk].at[pl.ds(block * OWN, OWN)]
        side = 0 if direction > 0 else 1
        pltpu.make_async_remote_copy(
            src_ref=place_of,
            dst_ref=place_of,
            send_sem=ag_send.at[chunk, side, hop - 1],
            recv_sem=ag_recv.at[chunk, side, hop - 1],
            device_id=ring_device((z + direction + NZ) % NZ),
            device_id_type=MESH,
        ).wait_recv()

    def start_ring(first):
        for chunk in (first, first + 1):
            for direction in (1, -1):
                ring_copy(chunk, direction, 1).start()

    def forward_ring(first, hop):
        for chunk in (first, first + 1):
            for direction in (1, -1):
                ring_arrival(chunk, direction, hop - 1)
                if hop <= hops(chunk, direction):
                    ring_copy(chunk, direction, hop).start()

    start_ring(0)

    row = cells[...]
    owner = row >> 1
    from_q = (owner >> 5) * NX + (owner & 3)
    entry = ((owner >> 2) & 7) * 4 + (iota(row.shape, 1) >> 5) * 2 + (row & 1)
    code_row = (from_q * 32 + entry).astype(F32)
    q_row = from_q.astype(F32)
    code_col = to_column(code_row)
    q_col = to_column(q_row)
    ahead = (q_col == q_row) & (code_col < code_row)
    rank = jnp.sum(jnp.where(ahead, 1.0, 0.0), axis=0, keepdims=True)
    over = jnp.where(jnp.max(rank, axis=1, keepdims=True) >= PLACES, 1, 0)
    at = q_row * PLACES + jnp.minimum(rank, PLACES - 1.0)
    tables[...] = jnp.zeros(tables.shape, I32)
    tables[0:1, 0 : MB * CELLS] = at.astype(I32)
    at_col = to_column(jnp.where(rank < PLACES, at, -1.0))
    spread = jnp.broadcast_to(at_col, (MB * CELLS, 256)) == iota((MB * CELLS, 256), 1).astype(F32)
    number = iota((MB * CELLS, 256), 0).astype(F32)
    back_row = jnp.sum(jnp.where(spread, number, 0.0), axis=0, keepdims=True)

    lane = iota((8, 128), 1)
    for zz in range(NZ):
        metas[zz] = jnp.where(lane == 64, jnp.broadcast_to(over, (8, 128)), meta[zz])
    metain[z] = metas[z]

    def meta_copy(step):
        there = (z + step) % NZ
        return pltpu.make_async_remote_copy(
            src_ref=metas.at[there],
            dst_ref=metain.at[z],
            send_sem=meta_send.at[step],
            recv_sem=meta_recv.at[step],
            device_id=ring_device(there),
            device_id_type=MESH,
        )

    for step in range(1, NZ):
        meta_copy(step).start()

    slots = pltpu.make_async_copy(tables, slot, local_sem.at[0])
    slots.start()

    for chunk in range(CHUNKS):
        ag[chunk][pl.ds(z * OWN, OWN)] = obj[:, chunk]

    forward_ring(0, 2)
    forward_ring(0, 3)
    start_ring(2)

    for step in range(1, NZ):
        meta_copy(step).wait()
    wanted = metain[:, 0, :].astype(F32)
    lanes = iota((NZ, 128), 1)
    column_over = jnp.max(
        jnp.max(jnp.where(lanes == 64, wanted, 0.0), axis=1, keepdims=True), axis=0, keepdims=True
    )
    mark[...] = jnp.broadcast_to(column_over, (8, 128)).astype(I32)
    marks[mine] = mark[...]

    def mark_copy(step):
        return pltpu.make_async_remote_copy(
            src_ref=mark,
            dst_ref=marks.at[mine],
            send_sem=mark_send.at[step],
            recv_sem=mark_recv.at[step],
            device_id=plane_device((mine + step) % PLANE),
            device_id_type=MESH,
        )

    valid = (wanted >= 0.0) & (lanes < 64)
    held = jnp.where(valid, 1.0, 0.0)
    big_row, big_lane = iota((128, 128), 0), iota((128, 128), 1)
    group = jnp.where((big_row >> 2) == (big_lane >> 2), 1.0, 0.0)
    before = jnp.where(((big_row >> 2) == (big_lane >> 2)) & (big_row < big_lane), 1.0, 0.0)
    in_group = jnp.dot(held, group, preferred_element_type=F32)
    order = jnp.dot(held, before, preferred_element_type=F32)
    rows = []
    running = jnp.zeros((1, 128), F32)
    for zz in range(NZ):
        rows.append(order[zz : zz + 1] + running)
        running = running + in_group[zz : zz + 1]
    order = jnp.concatenate(rows, axis=0)
    named = iota((NZ, 128), 0).astype(F32) * OWN + wanted + 1.0
    picks = [
        jnp.sum(jnp.where(valid & (order == float(k)), named, 0.0), axis=0, keepdims=True)
        for k in range(PLACES)
    ]
    picks.append(jnp.zeros((16 - PLACES, 128), F32))
    picks = jnp.dot(jnp.concatenate(picks, axis=0), group, preferred_element_type=F32)
    metas[0] = picks[0:8].astype(I32)
    metas[1] = picks[8:16].astype(I32)
    for half in range(2):
        pltpu.make_async_copy(metas.at[half], pick.at[half], local_sem.at[1 + half]).start()
    target = iota((1, 256), 1)
    target_q = quotient(target, PLACES, PLANE)
    target_k = target - target_q * PLACES
    chosen = jnp.where(
        iota((128, 256), 0) == jnp.broadcast_to(target_q * 4, (128, 256)), 1.0, 0.0
    )
    chosen = jnp.dot(picks, chosen, preferred_element_type=F32)
    here = (iota((16, 256), 0) == jnp.broadcast_to(target_k, (16, 256))) & (
        iota((16, 256), 1) < ROWS
    )
    sums_row = jnp.sum(jnp.where(here, chosen, 0.0), axis=0, keepdims=True)
    tab[...] = jnp.zeros(tab.shape, I32)
    tab[0:1, :] = back_row.astype(I32)
    tab[1:2, :] = sums_row.astype(I32)
    slots.wait()
    for half in range(2):
        pltpu.make_async_copy(metas.at[half], pick.at[half], local_sem.at[1 + half]).wait()
    for step in range(1, PLANE):
        mark_copy(step).start()

    forward_ring(0, 4)
    ring_arrival(0, 1, 4)
    ring_arrival(1, -1, 4)

    def plane_copy(chunk, step):
        q = (mine + step) % PLANE
        return pltpu.make_async_remote_copy(
            src_ref=pack.at[chunk, pl.ds(q * PLACES, PLACES)],
            dst_ref=recv[chunk].at[pl.ds(mine * PLACES, PLACES)],
            send_sem=xy_send.at[chunk, step],
            recv_sem=xy_recv.at[chunk, step],
            device_id=plane_device(q),
            device_id_type=MESH,
        )

    def send_plane(chunk):
        def fill(q, carry):
            for k in range(PLACES):
                index = jnp.clip(pick[k // 8, k % 8, q * 4], 1, COLUMN) - 1
                pack[chunk, q * PLACES + k] = ag[chunk][index]
            return carry

        lax.fori_loop(0, PLANE, fill, 0)

        def send(step, carry):
            plane_copy(chunk, step).start()
            return carry

        lax.fori_loop(1, PLANE, send, 0)
        recv[chunk][pl.ds(mine * PLACES, PLACES)] = pack[chunk, pl.ds(mine * PLACES, PLACES)]

    def pair_copy(part):
        return pltpu.make_async_remote_copy(
            src_ref=other.at[part],
            dst_ref=win.at[core, part],
            send_sem=pair_send.at[part],
            recv_sem=pair_recv.at[part],
            device_id=partner,
            device_id_type=MESH,
        )

    def take_plane(chunk):
        def arrive(step, carry):
            plane_copy(chunk, step).wait_recv()
            return carry

        lax.fori_loop(1, PLANE, arrive, 0)
        part, half = chunk // 2, chunk % 2

        def lay(r, carry):
            start = pl.multiple_of(r * PR + half * 8, 8)
            for column in range(2):
                k = r * 2 + column
                lanes_of = slice(column * PW, column * PW + PW)
                keep = jnp.clip(slot[0, core * CELLS + k], 0, ROWS - 1)
                give = jnp.clip(slot[0, (1 - core) * CELLS + k], 0, ROWS - 1)
                win[core, part, pl.ds(start, 8), lanes_of] = recv[chunk][keep]
                other[part, pl.ds(start, 8), lanes_of] = recv[chunk][give]
            return carry

        lax.fori_loop(0, W // PR, lay, 0)

    send_plane(0)
    send_plane(1)
    forward_ring(2, 2)
    forward_ring(2, 3)
    forward_ring(2, 4)
    ring_arrival(2, 1, 4)
    send_plane(2)
    ring_arrival(3, -1, 4)
    send_plane(3)
    take_plane(0)
    take_plane(1)
    pair_copy(0).start()
    for step in range(1, PLANE):
        mark_copy(step).wait()
    flag[...] = jnp.max(marks[...].astype(F32), axis=0).astype(I32)
    take_plane(2)
    take_plane(3)
    pair_copy(1).start()
    for chunk in range(CHUNKS):
        for direction in (1, -1):
            for hop in range(1, hops(chunk, direction) + 1):
                ring_copy(chunk, direction, hop).wait_send()

    def drain(step, carry):
        for chunk in range(CHUNKS):
            plane_copy(chunk, step).wait_send()
        return carry

    lax.fori_loop(1, PLANE, drain, 0)
    pair_copy(0).wait()
    pair_copy(1).wait()


def fetch_windows(owned, wanted, cells):
    vmem = pl.BlockSpec(memory_space=pltpu.VMEM)
    tile = (8, 128)
    return pl.pallas_call(
        gather_kernel,
        out_shape=(
            jax.ShapeDtypeStruct((2, 2, W, W), F32),
            jax.ShapeDtypeStruct((8, 256), I32),
            jax.ShapeDtypeStruct(tile, I32),
        ),
        in_specs=[vmem] * 3,
        out_specs=(vmem, vmem, vmem),
        scratch_shapes=[
            [pltpu.VMEM((COLUMN,) + tile, F32)] * CHUNKS,
            pltpu.VMEM((NZ,) + tile, I32),
            pltpu.VMEM((NZ,) + tile, I32),
            pltpu.VMEM(tile, I32),
            pltpu.SMEM((2,) + tile, I32),
            pltpu.SMEM(tile, I32),
            pltpu.VMEM((CHUNKS, ROWS) + tile, F32),
            [pltpu.VMEM((ROWS,) + tile, F32)] * CHUNKS,
            pltpu.VMEM(tile, I32),
            pltpu.VMEM((PLANE,) + tile, I32),
            pltpu.VMEM((2, W, W), F32),
            pltpu.SemaphoreType.DMA((CHUNKS, 2, 4)),
            pltpu.SemaphoreType.DMA((CHUNKS, 2, 4)),
            pltpu.SemaphoreType.DMA((NZ,)),
            pltpu.SemaphoreType.DMA((NZ,)),
            pltpu.SemaphoreType.DMA((PLANE,)),
            pltpu.SemaphoreType.DMA((PLANE,)),
            pltpu.SemaphoreType.DMA((CHUNKS, PLANE)),
            pltpu.SemaphoreType.DMA((CHUNKS, PLANE)),
            pltpu.SemaphoreType.DMA((2,)),
            pltpu.SemaphoreType.DMA((2,)),
            pltpu.SemaphoreType.DMA((3,)),
        ],
        compiler_params=pltpu.CompilerParams(collective_id=0, has_side_effects=True),
        name="fetch_windows",
    )(owned, wanted, cells)


def parts(value):
    high = value.astype(BF16)
    return high, (value - high.astype(F32)).astype(BF16)


def from_left(real, imag, table, sign):
    high, low = parts(jnp.concatenate([real, imag], axis=1))
    out = jnp.dot(
        table[...], jnp.concatenate([high, low, high], axis=0), preferred_element_type=F32
    )
    return out[:W, :W] - sign * out[W:, W:], out[:W, W:] + sign * out[W:, :W]


def from_right(real, imag, table, sign):
    high, low = parts(jnp.concatenate([real, imag], axis=0))
    out = lax.dot_general(
        jnp.concatenate([high, low, high], axis=1),
        table[...],
        (((1,), (1,)), ((), ())),
        preferred_element_type=F32,
    )
    return out[:W, :W] - sign * out[W:, W:], sign * out[:W, W:] + out[W:, :W]


def both_sides(real, imag, table, sign):
    real, imag = from_left(real, imag, table, sign)
    return from_right(real, imag, table, sign)


def position_kernel(win, probe, measured, dft, move, grad):
    core = lax.axis_index("section")

    def lay(index, real, imag):
        for k in range(CELLS):
            rows = slice(k // 2 * PR, k // 2 * PR + PR)
            lanes = slice(k % 2 * PW, k % 2 * PW + PW)
            grad[index, k, 0] = real[rows, lanes]
            grad[index, k, 1] = imag[rows, lanes]

    pr, pi = probe[0], probe[1]
    ar, ai = win[0, 0], win[0, 1]
    wave_r, wave_i = both_sides(pr * ar - pi * ai, pr * ai + pi * ar, move, 1.0)
    br, bi = win[1, 0], win[1, 1]
    far_r, far_i = both_sides(
        wave_r * br - wave_i * bi, wave_r * bi + wave_i * br, dft, 1.0
    )
    gap = far_r * far_r + far_i * far_i - measured[core]
    back_r, back_i = both_sides(gap * far_r, gap * far_i, dft, -1.0)
    lay(1, wave_r * back_r + wave_i * back_i, wave_r * back_i - wave_i * back_r)
    br, bi = win[1, 0], win[1, 1]
    low_r, low_i = both_sides(
        br * back_r + bi * back_i, br * back_i - bi * back_r, move, -1.0
    )
    pr, pi = probe[0], probe[1]
    lay(0, pr * low_r + pi * low_i, pr * low_i - pi * low_r)


def position_gradients(windows, probe_wave, intensities, dft, move):
    vmem = pl.BlockSpec(memory_space=pltpu.VMEM)
    return pl.pallas_call(
        position_kernel,
        out_shape=jax.ShapeDtypeStruct((2, CELLS, 2, PR, PW), F32),
        in_specs=[vmem] * 5,
        out_specs=vmem,
        name="position_gradients",
    )(windows, probe_wave, intensities, dft, move)


def return_kernel(
    grad,
    back,
    tab,
    out,
    cells,
    pack,
    recv,
    total,
    ring,
    mix,
    pair_send,
    pair_recv,
    xy_send,
    xy_recv,
    rs_send,
    rs_recv,
):
    core, y, z, x = place()
    mine = y * NX + x
    barrier = pltpu.get_barrier_semaphore()

    def ring_device(zz):
        return (core, y * (NZ * NX) + zz * NX + x)

    def plane_device(q):
        return (core, plane_tile(q, z))

    def greet_plane(step, carry):
        pl.semaphore_signal(
            barrier, inc=1, device_id=plane_device((mine + step) % PLANE), device_id_type=MESH
        )
        return carry

    partner = (1 - core, y * (NZ * NX) + z * NX + x)
    for direction in (1, -1):
        pl.semaphore_signal(
            barrier,
            inc=1,
            device_id=ring_device((z + direction + NZ) % NZ),
            device_id_type=MESH,
        )
    lax.fori_loop(1, PLANE, greet_plane, 0)
    pl.semaphore_signal(barrier, inc=1, device_id=partner, device_id_type=MESH)
    pl.semaphore_wait(barrier, PLANE + 2)

    def pair_copy(chunk):
        return pltpu.make_async_remote_copy(
            src_ref=grad.at[1 - core, :, chunk],
            dst_ref=cells[chunk].at[pl.ds(core * CELLS, CELLS)],
            send_sem=pair_send.at[chunk],
            recv_sem=pair_recv.at[chunk],
            device_id=partner,
            device_id_type=MESH,
        )

    def pair_arrival(chunk):
        pltpu.make_async_remote_copy(
            src_ref=grad.at[1 - core, :, chunk],
            dst_ref=cells[chunk].at[pl.ds((1 - core) * CELLS, CELLS)],
            send_sem=pair_send.at[chunk],
            recv_sem=pair_recv.at[chunk],
            device_id=partner,
            device_id_type=MESH,
        ).wait_recv()

    for chunk in range(CHUNKS):
        pair_copy(chunk).start()
    for chunk in range(CHUNKS):
        cells[chunk][pl.ds(core * CELLS, CELLS)] = grad[core, :, chunk]
        recv[chunk, ROWS * 8 :] = jnp.zeros(((256 - ROWS) * 8, 128), F32)

    mix[...] = jnp.where(
        jnp.broadcast_to(tab[1:2, :], (COLUMN, 256)) == iota((COLUMN, 256), 0) + 1, 1.0, 0.0
    ).astype(BF16)

    def plane_copy(chunk, step):
        q = (mine + step) % PLANE
        return pltpu.make_async_remote_copy(
            src_ref=pack.at[chunk, pl.ds(q * (PLACES * 8), PLACES * 8)],
            dst_ref=recv.at[chunk, pl.ds(mine * (PLACES * 8), PLACES * 8)],
            send_sem=xy_send.at[chunk, step],
            recv_sem=xy_recv.at[chunk, step],
            device_id=plane_device(q),
            device_id_type=MESH,
        )

    for chunk in range(CHUNKS):
        pair_arrival(chunk)

        def fill(q, carry):
            for k in range(PLACES):
                row = q * PLACES + k
                pack[chunk, pl.ds(pl.multiple_of(row * 8, 8), 8)] = cells[chunk][
                    jnp.clip(back[0, row], 0, MB * CELLS - 1)
                ]
            return carry

        lax.fori_loop(0, PLANE, fill, 0)

        def send(step, carry):
            plane_copy(chunk, step).start()
            return carry

        lax.fori_loop(1, PLANE, send, 0)
        own_rows = pl.ds(mine * (PLACES * 8), PLACES * 8)
        recv[chunk, own_rows] = pack[chunk, own_rows]

    def block(zz):
        return pl.ds(((zz + 2 * NZ) % NZ) * (OWN * 8), OWN * 8)

    def ring_copy(chunk, direction, step):
        side = 0 if direction > 0 else 1
        reach = hops(chunk, direction)
        return pltpu.make_async_remote_copy(
            src_ref=total.at[chunk, block(z + direction * reach)]
            if step == 1
            else ring.at[chunk, side, step - 2],
            dst_ref=ring.at[chunk, side, step - 1],
            send_sem=rs_send.at[chunk, side, step - 1],
            recv_sem=rs_recv.at[chunk, side, step - 1],
            device_id=ring_device((z + direction + NZ) % NZ),
            device_id_type=MESH,
        )

    def sum_cells(chunk):
        def arrive(step, carry):
            plane_copy(chunk, step).wait_recv()
            return carry

        lax.fori_loop(1, PLANE, arrive, 0)

        def add(r, carry):
            high, low = parts(recv[chunk, pl.ds(r, 256, stride=8), :])
            both = jnp.dot(
                mix[...], jnp.concatenate([high, low], axis=1), preferred_element_type=F32
            )
            total[chunk, pl.ds(r, COLUMN, stride=8), :] = both[:, :128] + both[:, 128:]
            return carry

        lax.fori_loop(0, 8, add, 0)
        for direction in (1, -1):
            ring_copy(chunk, direction, 1).start()

    def pass_on(chunk, step):
        for direction in (1, -1):
            reach = hops(chunk, direction)
            side = 0 if direction > 0 else 1
            if step <= reach:
                ring_copy(chunk, direction, step - 1).wait_recv()
                ring[chunk, side, step - 2] += total[
                    chunk, block(z + direction * (reach - step + 1))
                ]
                ring_copy(chunk, direction, step).start()

    def finish(chunk):
        value = total[chunk, block(z)]
        for direction in (1, -1):
            reach = hops(chunk, direction)
            side = 0 if direction > 0 else 1
            ring_copy(chunk, direction, reach).wait_recv()
            value = value + ring[chunk, side, reach - 1]
        out[:, chunk] = value.reshape(OWN, 8, 128)

    sum_cells(0)
    sum_cells(1)
    pass_on(0, 2)
    pass_on(1, 2)
    sum_cells(2)
    pass_on(0, 3)
    pass_on(1, 3)
    sum_cells(3)
    pass_on(0, 4)
    pass_on(1, 4)
    pass_on(2, 2)
    pass_on(3, 2)
    finish(0)
    finish(1)
    pass_on(2, 3)
    pass_on(3, 3)
    pass_on(2, 4)
    pass_on(3, 4)
    finish(2)
    finish(3)

    for chunk in range(CHUNKS):
        pair_copy(chunk).wait_send()
        for direction in (1, -1):
            for step in range(1, hops(chunk, direction) + 1):
                ring_copy(chunk, direction, step).wait_send()

    def drain(step, carry):
        for chunk in range(CHUNKS):
            plane_copy(chunk, step).wait_send()
        return carry

    lax.fori_loop(1, PLANE, drain, 0)


def return_gradients(gradients, table):
    vmem = pl.BlockSpec(memory_space=pltpu.VMEM)
    smem = pl.BlockSpec(memory_space=pltpu.SMEM)
    tile = (8, 128)
    return pl.pallas_call(
        return_kernel,
        out_shape=jax.ShapeDtypeStruct((OWN, CHUNKS) + tile, F32),
        in_specs=[vmem, smem, vmem],
        out_specs=vmem,
        scratch_shapes=[
            [pltpu.VMEM((MB * CELLS,) + tile, F32)] * CHUNKS,
            pltpu.VMEM((CHUNKS, ROWS * 8, 128), F32),
            pltpu.VMEM((CHUNKS, 256 * 8, 128), F32),
            pltpu.VMEM((CHUNKS, COLUMN * 8, 128), F32),
            pltpu.VMEM((CHUNKS, 2, 4, OWN * 8, 128), F32),
            pltpu.VMEM((COLUMN, 256), BF16),
            pltpu.SemaphoreType.DMA((CHUNKS,)),
            pltpu.SemaphoreType.DMA((CHUNKS,)),
            pltpu.SemaphoreType.DMA((CHUNKS, PLANE)),
            pltpu.SemaphoreType.DMA((CHUNKS, PLANE)),
            pltpu.SemaphoreType.DMA((CHUNKS, 2, 4)),
            pltpu.SemaphoreType.DMA((CHUNKS, 2, 4)),
        ],
        compiler_params=pltpu.CompilerParams(collective_id=1, has_side_effects=True),
        name="return_gradients",
    )(gradients, table[0:1], table)


def swapped(block):
    return lax.ppermute(block, "section", [(0, 1), (1, 0)])


def full_windows(owned, send_plan, cell_slot):
    core = lax.axis_index("section")
    outbound = jnp.swapaxes(send_plan, 0, 1)
    patches = owned[jnp.maximum(outbound, 0)]
    arrived = lax.all_to_all(patches, "tile", split_axis=0, concat_axis=0, tiled=True)
    windows = []
    for batch in range(MB):
        flat = arrived[:, batch].reshape((-1, 2, PR, PW))
        picked = flat[cell_slot[batch]].reshape(W // PR, W // PW, 2, PR, PW)
        windows.append(jnp.transpose(picked, (2, 0, 3, 1, 4)).reshape(2, W, W))
    windows = jnp.stack(windows)
    passed = swapped(lax.dynamic_index_in_dim(windows, 1 - core, 0, keepdims=False))
    kept = lax.dynamic_index_in_dim(windows, core, 0, keepdims=False)
    first = core == 0
    return jnp.stack([jnp.where(first, kept, passed), jnp.where(first, passed, kept)])


def full_sums(gradients, send_plan, cell_slot):
    core = lax.axis_index("section")
    passed = swapped(lax.dynamic_index_in_dim(gradients, 1 - core, 0, keepdims=False))
    kept = lax.dynamic_index_in_dim(gradients, core, 0, keepdims=False)
    first = core == 0
    batches = [jnp.where(first, kept, passed), jnp.where(first, passed, kept)]
    slots = 2 * NX * NY * NZ
    placed = [
        jnp.zeros((slots, 2, PR, PW), F32)
        .at[cell_slot[batch]]
        .set(batches[batch])
        .reshape(slots // 2, 2, 2, PR, PW)
        for batch in range(MB)
    ]
    returned = lax.all_to_all(
        jnp.stack(placed, axis=1), "tile", split_axis=0, concat_axis=0, tiled=True
    )
    outbound = jnp.swapaxes(send_plan, 0, 1)
    target = jnp.where(outbound < 0, OWN, outbound).reshape(-1)
    sums = jax.ops.segment_sum(
        returned.reshape((-1, 2, PR, PW)), target, num_segments=OWN + 1
    )
    return sums[:OWN]


def body(dft, move, object_slices, probe_wave, intensities, send_list, cell_slot):
    owned = object_slices[0]
    send_plan = send_list[0]
    wanted = jnp.transpose(send_plan.reshape(MB, NY, NZ, NX, 2), (2, 1, 3, 0, 4))
    wanted = jnp.pad(wanted.reshape(NZ, 1, 64), ((0, 0), (0, 0), (0, 64)))
    wanted = jnp.broadcast_to(wanted, (NZ, 8, 128))
    windows, table, flag = fetch_windows(
        owned.reshape(OWN, CHUNKS, 8, 128), wanted, cell_slot.reshape(1, MB * CELLS)
    )
    crowded = flag[0, 0] > 0
    windows = lax.cond(
        crowded,
        lambda: full_windows(owned, send_plan, cell_slot),
        lambda: windows,
    )
    gradients = position_gradients(windows, probe_wave, intensities, dft, move)
    sums = lax.cond(
        crowded,
        lambda: full_sums(gradients, send_plan, cell_slot),
        lambda: return_gradients(
            gradients.reshape(2, CELLS, CHUNKS, 8, 128), table
        ).reshape(OWN, 2, PR, PW),
    )
    return sums[None]


def solution(mesh):
    dft, move = matrix_tables()
    in_specs = (
        P("section", "tile", None, None, None),
        P(),
        P("tile", None, None),
        P("tile", None, None, None),
        P("tile", None),
    )
    out_specs = P("section", "tile", None, None, None)
    step = functools.partial(body, jnp.asarray(dft), jnp.asarray(move))
    return jax.shard_map(step, mesh=mesh, in_specs=in_specs, out_specs=out_specs, check_vma=False)
```

time: 564 us -> 178 us (0.32); the launches traced: 555 us -> 177 us
  waiting for transfers between devices: 368 us -> 0 us
  Pallas kernels: 0 us -> 169 us
  other arithmetic: 78.6 us -> 0 us
  starting transfers between devices: 39.4 us -> 0 us
  matrix products: 26 us -> 0 us
  local copies, waits for them, and re-layouts: 31.2 us -> 7.35 us
  loops' own time: 11.5 us -> 0.21 us
    all_to_all x2 -> x0, waiting for transfers between devices: 363 us -> none  [the longest x1 183 us: body(): lax.all_to_all(pick_patches(owned_blocks, outbound), 'tile', split_axis=0...]
    pallas_call x0 -> x3, Pallas kernels: none -> 169 us  [the longest x1 82.8 us: fetch_windows(): pl.pallas_call(gather_kernel, out_shape=(jax.ShapeDtypeStruct((2, 2, W, W...]
    scatter-add x3 -> x0, other arithmetic: 54 us -> none  [the longest x1 45.4 us: accumulate(): jax.ops.segment_sum(flattened, target, num_segments=block_count + 1)]
    dot_general x16 -> x0, matrix products: 26 us -> none  [the longest x4 7.28 us: transform(): sine_part = jnp.einsum('cpij,jk->cpik', middle, signed, precision=highest)]
    all_to_all x2 -> x0, starting transfers between devices: 24.2 us -> none  [the longest x1 15.6 us: body(): lax.all_to_all(pick_patches(owned_blocks, outbound), 'tile', split_axis=0...]
    ppermute x2 -> x0, starting transfers between devices: 15.3 us -> none  [swapped(): return lax.ppermute(block, axis, route)]
    another operation x3 -> x2, loops' own time: 11.5 us -> 0.21 us  [the longest x1 0.19 us: body(): lax.cond(crowded, lambda: full_windows(owned, send_plan, cell_slot), lamb...]
    gather x3 -> x0, local copies, waits for them, and re-layouts: 9.98 us -> none  [the longest x2 5.53 us: slot_table(): return stitch(flattened[slot_ids])]
  transfers between devices with their start and end apart: 4 -> 0, of which waited for: 4 -> 0; matrix products, arithmetic and copies ran while one was open for 1% -> 0% of each run, Pallas kernels for 0% -> 0%
where the time goes in v1:
time: 178 us; the launch traced here: 177 us
  Pallas kernels  169 us (95%)
  local copies, waits for them, and re-layouts  7.35 us (4%)
    pallas_call x1, Pallas kernels, fetch_windows(): pl.pallas_call(gather_kernel, out_shape=(jax.ShapeDtypeStruct((2, 2, W, W...  82.8 us
    pallas_call x1, Pallas kernels, return_gradients(): pl.pallas_call(return_kernel, out_shape=jax.ShapeDtypeStruct((OWN, CHUNKS...  78.5 us
    pallas_call x1, Pallas kernels, position_gradients(): pl.pallas_call(position_kernel, out_shape=jax.ShapeDtypeStruct((2, CELLS,...  7.84 us

profile of v1, /device:TPU:32, one launch (start us, length us, event | category | flops | bytes accessed | tf_op | source)
XLA Modules:
  0.0 177.4 jit_solution(16711648167576179906)
XLA Ops:
  0.0 0.8 reshape_squeeze.7
  0.8 0.2 copy.16
  1.0 0.1 copy.17
  1.0 0.6 broadcast_in_dim.26.meta
  1.7 1.3 reshape.152.cells
  3.0 82.8 %fetch_windows.1 = (f32[2,2,256,256]{3,2,1,0:T(8,128)S(1)}, s32[8,256]{1,0:T(8,128)S(1)}, s32[8,128]{1,0:T(8,128)}) custom-call(f32[32,4,8,128]{3,2,1,0:T(8,128)} %bitcast.64, s32[8,8,128]{2,1,0:T(8,128)} %broadcast_in_dim.26.meta, s32[1,64]{1,0:T(1,128)} %reshape.152.cells), custom_call_target="tpu_custom_call" | custom-call | tf_op jit(solution)/shard_map/fetch_windows/pallas_call | solution.py:391
  85.8 1.2 slice.27
  87.6 0.8 copy.18
  88.4 0.2 conditional.2
  88.6 0.0 copy-start
  88.7 1.0 copy-done
  89.6 0.0 copy-start.1
  89.6 7.8 %position_gradients.1 = f32[2,32,2,16,128]{4,3,2,1,0:T(8,128)S(1)} custom-call(f32[2,2,256,256]{3,2,1,0:T(8,128)} %copy-done, f32[2,256,256]{2,1,0:T(8,128)} %probe.1, f32[2,256,256]{2,1,0:T(8,128)} %measured.1, bf16[512,768]{1,0:T(8,128)(2,1)} %constant.61.clone.dft, bf16[512,768]{1,0:T(8,128)(2,1)} %constant.62.clone.move), custom_call_target="tpu_custom_call" | custom-call | tf_op jit(solution)/shard_map/position_gradients/pallas_call | solution.py:488
  97.5 0.0 copy-done.1
  97.5 79.1 %conditional.3 = (f32[1,32,2,16,128]{4,3,2,1,0:T(8,128)S(1)}) conditional(s32[]{:T(128)} %bitcast.36, (f32[2,32,2,16,128]{4,3,2,1,0:T(8,128)S(1)}, s32[8,256]{1,0:T(8,128)S(1)}) %tuple.20, (s32[2,128,2]{2,0,1:T(2,128)S(1)}, s32[2,32]{1,0:T(2,128)S(1)}, f32[2,32,2,16,128]{4,3,2,1,0:T(8,128)S(1)}) %tuple.36), branch_computations={%region_2.3_spmd, %region_3.7_spmd} | conditional | flops 4457675 | bytes 85486560 | solution.py:786
  97.5 0.6 slice.22.back
  98.1 78.5 %return_gradients.1 = f32[32,4,8,128]{3,2,1,0:T(8,128)S(1)} custom-call(f32[2,32,4,8,128]{4,3,2,1,0:T(8,128)S(1)} %bitcast.69, s32[1,256]{1,0:T(1,128)} %slice.22.back, s32[8,256]{1,0:T(8,128)S(1)} %get-tuple-element.34.tab), custom_call_target="tpu_custom_call" | custom-call | tf_op jit(solution)/shard_map/cond/branch_0_fun/return_gradients/pallas_call | solution.py:700
  176.6 0.8 copy.28
  (1 shorter events, 0.0 us)
Async XLA Ops:
  88.6 1.0 copy-start
  89.6 7.9 %copy-start.1 = (s32[2,32]{1,0:T(2,128)S(1)}, s32[2,32]{1,0:T(2,128)}, u32[]{:S(2)}) copy-start(s32[2,32]{1,0:T(2,128)} %param.15) | copy-start | bytes 772

commit v2 on v1

v2 whole, which is shorter than its diff:
```python
import functools

import jax
import jax.numpy as jnp
import ml_dtypes
import numpy as np
from jax import lax
from jax.experimental import pallas as pl
from jax.experimental.pallas import tpu as pltpu
from jax.sharding import PartitionSpec as P

W = 256
PW = 128
PR = 16
MB = 2
CELLS = 32
NX, NY, NZ = 4, 4, 8
PLANE = NX * NY
OWN = 32
COLUMN = NZ * OWN
PLACES = 32
ROWS = 4 * PLACES
CHUNKS = 4
PHASE_SCALE = 20.0
MESH = pl.DeviceIdType.MESH
F32 = jnp.float32
I32 = jnp.int32
BF16 = jnp.bfloat16


def stacked_parts(matrix):
    rows = np.concatenate([matrix.real, matrix.imag], axis=0).astype(np.float32)
    high = rows.astype(ml_dtypes.bfloat16)
    low = (rows - high.astype(np.float32)).astype(ml_dtypes.bfloat16)
    return np.concatenate([high, high, low], axis=1)


def matrix_tables():
    index = np.arange(W)
    product = np.outer(index, index) % W
    dft = np.exp(-2j * np.pi * product / W) / np.sqrt(W)
    frequency = np.where(index < W // 2, index, index - W).astype(np.float64)
    diagonal = np.exp(-1j * PHASE_SCALE * frequency**2 / (W * W))
    move = np.conj(dft) @ (diagonal[:, None] * dft)
    move = (move + move.T) / 2
    return stacked_parts(dft), stacked_parts(move)


def place():
    tile = lax.axis_index("tile")
    core = lax.axis_index("section")
    y = tile // (NZ * NX)
    z = (tile // NX) % NZ
    x = tile % NX
    return core, y, z, x


def device(core, y, z, x):
    return (core, y * (NZ * NX) + z * NX + x)


def iota(shape, axis):
    return lax.broadcasted_iota(I32, shape, axis)


def to_column(row):
    n = row.shape[1]
    wide = jnp.broadcast_to(row, (n, n))
    return jnp.sum(jnp.where(iota((n, n), 0) == iota((n, n), 1), wide, 0.0), axis=1, keepdims=True)


def exclusive(column):
    rows = [jnp.zeros_like(column[0:1])]
    for step in range(column.shape[0] - 1):
        rows.append(rows[-1] + column[step : step + 1])
    return jnp.concatenate(rows, axis=0)


def send_to(src, dst, send_sem, recv_sem, target):
    return pltpu.make_async_remote_copy(
        src_ref=src,
        dst_ref=dst,
        send_sem=send_sem,
        recv_sem=recv_sem,
        device_id=target,
        device_id_type=MESH,
    )


def greet(barrier, targets):
    for target in targets:
        pl.semaphore_signal(barrier, inc=1, device_id=target, device_id_type=MESH)
    pl.semaphore_wait(barrier, len(targets))


def hops(chunk, direction):
    return 4 if (chunk % 2 == 0) == (direction > 0) else 3


def gather_kernel(
    obj,
    meta,
    cells,
    win,
    tab,
    flag,
    ag,
    metas,
    metain,
    tables,
    pick,
    turn,
    slot,
    x_pack,
    x_recv,
    y_pack,
    y_recv,
    mark,
    marks_x,
    marks_y,
    marks_z,
    other,
    ag_send,
    ag_recv,
    meta_send,
    meta_recv,
    mark_send,
    mark_recv,
    x_send,
    x_sem,
    y_send,
    y_sem,
    pair_send,
    pair_recv,
    local_sem,
):
    core, y, z, x = place()
    partner = device(1 - core, y, z, x)

    def ring_device(step):
        return device(core, y, (z + step) % NZ, x)

    def x_device(step):
        return device(core, y, z, (x + step) % NX)

    def y_device(step):
        return device(core, (y + step) % NY, z, x)

    greet(
        pltpu.get_barrier_semaphore(),
        [ring_device(step) for step in range(1, NZ)]
        + [x_device(step) for step in range(1, NX)]
        + [y_device(step) for step in range(1, NY)]
        + [partner],
    )

    def block(chunk, zz):
        return ag[chunk].at[pl.ds(((zz + 2 * NZ) % NZ) * OWN, OWN)]

    def ring_copy(chunk, direction, hop):
        side = 0 if direction > 0 else 1
        held = block(chunk, z - direction * (hop - 1))
        return send_to(
            obj.at[:, chunk] if hop == 1 else held,
            held,
            ag_send.at[chunk, side, hop - 1],
            ag_recv.at[chunk, side, hop - 1],
            ring_device(direction + NZ),
        )

    def ring_arrival(chunk, direction, hop):
        side = 0 if direction > 0 else 1
        held = block(chunk, z - direction * hop)
        send_to(
            held,
            held,
            ag_send.at[chunk, side, hop - 1],
            ag_recv.at[chunk, side, hop - 1],
            ring_device(direction + NZ),
        ).wait_recv()

    def start_ring(first):
        for chunk in (first, first + 1):
            for direction in (1, -1):
                ring_copy(chunk, direction, 1).start()

    def forward_ring(first, hop):
        for chunk in (first, first + 1):
            for direction in (1, -1):
                ring_arrival(chunk, direction, hop - 1)
                if hop <= hops(chunk, direction):
                    ring_copy(chunk, direction, hop).start()

    start_ring(0)

    row = cells[...]
    owner = row >> 1
    entry = ((owner >> 2) & 7) * 4 + (iota(row.shape, 1) >> 5) * 2 + (row & 1)
    code_row = ((owner >> 5) * 128 + (owner & 3) * 32 + entry).astype(F32)
    y_row = (owner >> 5).astype(F32)
    code_col = to_column(code_row)
    y_col = to_column(y_row)
    ahead = (y_col == y_row) & (code_col < code_row)
    rank = jnp.sum(jnp.where(ahead, 1.0, 0.0), axis=0, keepdims=True)
    over = jnp.where(jnp.max(rank, axis=1, keepdims=True) >= PLACES, 1, 0)
    at = y_row * PLACES + jnp.minimum(rank, PLACES - 1.0)
    tables[0] = jnp.zeros((8, 128), I32)
    tables[0, 0:1, 0 : MB * CELLS] = at.astype(I32)
    at_col = to_column(jnp.where(rank < PLACES, at, -1.0))
    spread = jnp.broadcast_to(at_col, (MB * CELLS, ROWS)) == iota((MB * CELLS, ROWS), 1).astype(
        F32
    )
    number = iota((MB * CELLS, ROWS), 0).astype(F32)
    back_row = jnp.sum(jnp.where(spread, number, 0.0), axis=0, keepdims=True)

    lane = iota((8, 128), 1)
    for zz in range(NZ):
        metas[zz] = jnp.where(lane == 64, jnp.broadcast_to(over, (8, 128)), meta[zz])
    metain[z] = metas[z]

    def meta_copy(step):
        return send_to(
            metas.at[(z + step) % NZ],
            metain.at[z],
            meta_send.at[step],
            meta_recv.at[step],
            ring_device(step),
        )

    for step in range(1, NZ):
        meta_copy(step).start()

    def table_copy(index, target):
        return pltpu.make_async_copy(tables.at[index], target, local_sem.at[index])

    table_copy(0, slot).start()

    for chunk in range(CHUNKS):
        ag[chunk][pl.ds(z * OWN, OWN)] = obj[:, chunk]

    forward_ring(0, 2)
    forward_ring(0, 3)
    start_ring(2)

    for step in range(1, NZ):
        meta_copy(step).wait()
    wanted = metain[:, 0, :].astype(F32)
    lanes = iota((NZ, 128), 1)
    valid = (wanted >= 0.0) & (lanes < 64)
    held = jnp.where(valid, 1.0, 0.0)
    big_row, big_lane = iota((128, 128), 0), iota((128, 128), 1)
    one_device = (big_row >> 2) == (big_lane >> 2)
    one_x = ((big_row >> 2) & 3) == ((big_lane >> 2) & 3)
    group = jnp.where(one_device, 1.0, 0.0)
    before = jnp.where(one_device & (big_row < big_lane), 1.0, 0.0)
    column = jnp.where(one_x & (big_row < 64), 1.0, 0.0)
    above = jnp.where(one_x & ((big_row >> 4) < (big_lane >> 4)), 1.0, 0.0)
    in_group = jnp.dot(held, group, preferred_element_type=F32)
    order = jnp.dot(held, before, preferred_element_type=F32) + exclusive(in_group)
    in_all = jnp.sum(held, axis=0, keepdims=True)
    sums = jnp.concatenate([in_all, jnp.zeros((7, 128), F32)], axis=0)
    count = jnp.dot(sums, group, preferred_element_type=F32)[0:1]
    start = jnp.dot(sums, above, preferred_element_type=F32)[0:1]
    whole = jnp.dot(sums, column, preferred_element_type=F32)[0:1]
    order = order + start
    named = iota((NZ, 128), 0).astype(F32) * OWN + wanted + 1.0
    picks = [
        jnp.sum(jnp.where(valid & (order == float(k)), named, 0.0), axis=0, keepdims=True)
        for k in range(PLACES)
    ]
    picks = jnp.dot(jnp.concatenate(picks, axis=0), column, preferred_element_type=F32)
    for part in range(PLACES // 8):
        tables[1 + part] = picks[part * 8 : part * 8 + 8].astype(I32)
        table_copy(1 + part, pick.at[part]).start()
    over_x = jnp.where(jnp.max(whole, axis=1, keepdims=True) > PLACES, 1.0, 0.0)
    over_z = jnp.max(
        jnp.max(jnp.where(lanes == 64, wanted, 0.0), axis=1, keepdims=True), axis=0, keepdims=True
    )
    over = jnp.broadcast_to(jnp.maximum(over_x, over_z), (1, 128))
    mark[0] = jnp.concatenate([count, start, over, jnp.zeros((5, 128), F32)], axis=0).astype(I32)
    marks_x[x] = mark[0]

    def mark_copy(kind, step):
        targets = (x_device, y_device, ring_device)
        arrays = (marks_x, marks_y, marks_z)
        own = (x, y, z)
        return send_to(
            mark.at[kind],
            arrays[kind].at[own[kind]],
            mark_send.at[kind, step],
            mark_recv.at[kind, step],
            targets[kind](step),
        )

    for step in range(1, NX):
        mark_copy(0, step).start()
    target = iota((128, ROWS), 1)
    chosen = jnp.where(iota((128, ROWS), 0) == (target // PLACES) * 4, 1.0, 0.0)
    chosen = jnp.dot(picks, chosen, preferred_element_type=F32)
    here = iota((PLACES, ROWS), 0) == iota((PLACES, ROWS), 1) % PLACES
    sums_row = jnp.sum(jnp.where(here, chosen, 0.0), axis=0, keepdims=True)
    tab[...] = jnp.zeros(tab.shape, I32)
    tab[0:1, :] = back_row.astype(I32)
    tab[1:2, :] = sums_row.astype(I32)

    table_copy(0, slot).wait()
    for part in range(PLACES // 8):
        table_copy(1 + part, pick.at[part]).wait()

    forward_ring(0, 4)
    ring_arrival(0, 1, 4)
    ring_arrival(1, -1, 4)

    def x_copy(chunk, step):
        return send_to(
            x_pack.at[chunk, pl.ds(((x + step) % NX) * PLACES, PLACES)],
            x_recv[chunk].at[pl.ds(x * PLACES, PLACES)],
            x_send.at[chunk, step],
            x_sem.at[chunk, step],
            x_device(step),
        )

    def y_copy(chunk, step):
        return send_to(
            y_pack.at[chunk, pl.ds(((y + step) % NY) * PLACES, PLACES)],
            y_recv[chunk].at[pl.ds(y * PLACES, PLACES)],
            y_send.at[chunk, step],
            y_sem.at[chunk, step],
            y_device(step),
        )

    def along_x(chunk):
        def fill(to, carry):
            for k in range(PLACES):
                index = jnp.clip(pick[k // 8, k % 8, to * 4], 1, COLUMN) - 1
                x_pack[chunk, to * PLACES + k] = ag[chunk][index]
            return carry

        lax.fori_loop(0, NX, fill, 0)
        for step in range(1, NX):
            x_copy(chunk, step).start()
        own = pl.ds(x * PLACES, PLACES)
        x_recv[chunk][own] = x_pack[chunk, own]

    def along_y(chunk):
        for step in range(1, NX):
            x_copy(chunk, step).wait_recv()

        def fill(to, carry):
            for k in range(PLACES):
                index = jnp.clip(turn[to, k], 1, ROWS) - 1
                y_pack[chunk, to * PLACES + k] = x_recv[chunk][index]
            return carry

        lax.fori_loop(0, NY, fill, 0)
        for step in range(1, NY):
            y_copy(chunk, step).start()
        own = pl.ds(y * PLACES, PLACES)
        y_recv[chunk][own] = y_pack[chunk, own]

    def pair_copy(part):
        return send_to(
            other.at[part],
            win.at[core, part],
            pair_send.at[part],
            pair_recv.at[part],
            partner,
        )

    def take(chunk):
        for step in range(1, NY):
            y_copy(chunk, step).wait_recv()
        part, half = chunk // 2, chunk % 2

        def lay(r, carry):
            first = pl.multiple_of(r * PR + half * 8, 8)
            for side in range(2):
                k = r * 2 + side
                lanes_of = slice(side * PW, side * PW + PW)
                keep = jnp.clip(slot[0, core * CELLS + k], 0, ROWS - 1)
                give = jnp.clip(slot[0, (1 - core) * CELLS + k], 0, ROWS - 1)
                win[core, part, pl.ds(first, 8), lanes_of] = y_recv[chunk][keep]
                other[part, pl.ds(first, 8), lanes_of] = y_recv[chunk][give]
            return carry

        lax.fori_loop(0, W // PR, lay, 0)

    along_x(0)
    along_x(1)

    for step in range(1, NX):
        mark_copy(0, step).wait()
    counts = marks_x[:, 0, :].astype(F32)
    starts = marks_x[:, 1, :].astype(F32)
    four = iota((NX, 128), 1)
    wide = four.astype(F32)
    giver = iota((NX, 128), 0).astype(F32)
    onward = []
    back = jnp.zeros((NX, 128), F32)
    for to in range(NY):
        mine = four == to * 16 + x * 4
        many = jnp.sum(jnp.where(mine, counts, 0.0), axis=1, keepdims=True)
        low = jnp.sum(jnp.where(mine, starts, 0.0), axis=1, keepdims=True)
        first = exclusive(many)
        inside = (wide >= first) & (wide < first + many)
        onward.append(
            jnp.sum(
                jnp.where(inside, giver * PLACES + low + wide - first + 1.0, 0.0),
                axis=0,
                keepdims=True,
            )
        )
        inside = (wide >= low) & (wide < low + many)
        back = back + jnp.where(inside, to * PLACES + first + wide - low + 1.0, 0.0)
    last = 1 + PLACES // 8
    tables[last] = jnp.concatenate(onward + [jnp.zeros((4, 128), F32)], axis=0).astype(I32)
    table_copy(last, turn).start()
    tab[8:12, :] = back.astype(I32)
    mark[1] = jnp.broadcast_to(
        jnp.max(marks_x[:, 2, :].astype(F32), axis=0, keepdims=True), (8, 128)
    ).astype(I32)
    marks_y[y] = mark[1]
    for step in range(1, NY):
        mark_copy(1, step).start()
    table_copy(last, turn).wait()

    forward_ring(2, 2)
    along_y(0)
    forward_ring(2, 3)
    along_y(1)
    for step in range(1, NY):
        mark_copy(1, step).wait()
    mark[2] = jnp.max(marks_y[...].astype(F32), axis=0).astype(I32)
    marks_z[z] = mark[2]
    for step in range(1, NZ):
        mark_copy(2, step).start()
    forward_ring(2, 4)
    ring_arrival(2, 1, 4)
    along_x(2)
    ring_arrival(3, -1, 4)
    along_x(3)
    take(0)
    take(1)
    pair_copy(0).start()
    for step in range(1, NZ):
        mark_copy(2, step).wait()
    flag[...] = jnp.max(marks_z[...].astype(F32), axis=0).astype(I32)
    along_y(2)
    along_y(3)
    take(2)
    take(3)
    pair_copy(1).start()
    for chunk in range(CHUNKS):
        for direction in (1, -1):
            for hop in range(1, hops(chunk, direction) + 1):
                ring_copy(chunk, direction, hop).wait_send()
        for step in range(1, NX):
            x_copy(chunk, step).wait_send()
            y_copy(chunk, step).wait_send()
    pair_copy(0).wait()
    pair_copy(1).wait()


def fetch_windows(owned, wanted, cells):
    vmem = pl.BlockSpec(memory_space=pltpu.VMEM)
    tile = (8, 128)
    dma = pltpu.SemaphoreType.DMA
    return pl.pallas_call(
        gather_kernel,
        out_shape=(
            jax.ShapeDtypeStruct((2, 2, W, W), F32),
            jax.ShapeDtypeStruct((16, 128), I32),
            jax.ShapeDtypeStruct(tile, I32),
        ),
        in_specs=[vmem] * 3,
        out_specs=(vmem, vmem, vmem),
        scratch_shapes=[
            [pltpu.VMEM((COLUMN,) + tile, F32)] * CHUNKS,
            pltpu.VMEM((NZ,) + tile, I32),
            pltpu.VMEM((NZ,) + tile, I32),
            pltpu.VMEM((2 + PLACES // 8,) + tile, I32),
            pltpu.SMEM((PLACES // 8,) + tile, I32),
            pltpu.SMEM(tile, I32),
            pltpu.SMEM(tile, I32),
            pltpu.VMEM((CHUNKS, ROWS) + tile, F32),
            [pltpu.VMEM((ROWS,) + tile, F32)] * CHUNKS,
            pltpu.VMEM((CHUNKS, ROWS) + tile, F32),
            [pltpu.VMEM((ROWS,) + tile, F32)] * CHUNKS,
            pltpu.VMEM((3,) + tile, I32),
            pltpu.VMEM((NX,) + tile, I32),
            pltpu.VMEM((NY,) + tile, I32),
            pltpu.VMEM((NZ,) + tile, I32),
            pltpu.VMEM((2, W, W), F32),
            dma((CHUNKS, 2, 4)),
            dma((CHUNKS, 2, 4)),
            dma((NZ,)),
            dma((NZ,)),
            dma((3, NZ)),
            dma((3, NZ)),
            dma((CHUNKS, NX)),
            dma((CHUNKS, NX)),
            dma((CHUNKS, NY)),
            dma((CHUNKS, NY)),
            dma((2,)),
            dma((2,)),
            dma((2 + PLACES // 8,)),
        ],
        compiler_params=pltpu.CompilerParams(collective_id=0, has_side_effects=True),
        name="fetch_windows",
    )(owned, wanted, cells)


def parts(value):
    high = value.astype(BF16)
    return high, (value - high.astype(F32)).astype(BF16)


def from_left(real, imag, table, sign):
    high, low = parts(jnp.concatenate([real, imag], axis=1))
    out = jnp.dot(
        table[...], jnp.concatenate([high, low, high], axis=0), preferred_element_type=F32
    )
    return out[:W, :W] - sign * out[W:, W:], out[:W, W:] + sign * out[W:, :W]


def from_right(real, imag, table, sign):
    high, low = parts(jnp.concatenate([real, imag], axis=0))
    out = lax.dot_general(
        jnp.concatenate([high, low, high], axis=1),
        table[...],
        (((1,), (1,)), ((), ())),
        preferred_element_type=F32,
    )
    return out[:W, :W] - sign * out[W:, W:], sign * out[:W, W:] + out[W:, :W]


def both_sides(real, imag, table, sign):
    real, imag = from_left(real, imag, table, sign)
    return from_right(real, imag, table, sign)


def position_kernel(win, probe, measured, dft, move, grad):
    core = lax.axis_index("section")

    def lay(index, real, imag):
        for k in range(CELLS):
            rows = slice(k // 2 * PR, k // 2 * PR + PR)
            lanes = slice(k % 2 * PW, k % 2 * PW + PW)
            grad[index, k, 0] = real[rows, lanes]
            grad[index, k, 1] = imag[rows, lanes]

    pr, pi = probe[0], probe[1]
    ar, ai = win[0, 0], win[0, 1]
    wave_r, wave_i = both_sides(pr * ar - pi * ai, pr * ai + pi * ar, move, 1.0)
    br, bi = win[1, 0], win[1, 1]
    far_r, far_i = both_sides(
        wave_r * br - wave_i * bi, wave_r * bi + wave_i * br, dft, 1.0
    )
    gap = far_r * far_r + far_i * far_i - measured[core]
    back_r, back_i = both_sides(gap * far_r, gap * far_i, dft, -1.0)
    lay(1, wave_r * back_r + wave_i * back_i, wave_r * back_i - wave_i * back_r)
    br, bi = win[1, 0], win[1, 1]
    low_r, low_i = both_sides(
        br * back_r + bi * back_i, br * back_i - bi * back_r, move, -1.0
    )
    pr, pi = probe[0], probe[1]
    lay(0, pr * low_r + pi * low_i, pr * low_i - pi * low_r)


def position_gradients(windows, probe_wave, intensities, dft, move):
    vmem = pl.BlockSpec(memory_space=pltpu.VMEM)
    return pl.pallas_call(
        position_kernel,
        out_shape=jax.ShapeDtypeStruct((2, CELLS, 2, PR, PW), F32),
        in_specs=[vmem] * 5,
        out_specs=vmem,
        name="position_gradients",
    )(windows, probe_wave, intensities, dft, move)


def return_kernel(
    grad,
    places,
    tab,
    out,
    cells,
    y_pack,
    y_recv,
    x_pack,
    x_recv,
    total,
    ring,
    mix,
    pair_send,
    pair_recv,
    y_send,
    y_sem,
    x_send,
    x_sem,
    rs_send,
    rs_recv,
):
    core, y, z, x = place()
    partner = device(1 - core, y, z, x)

    def ring_device(step):
        return device(core, y, (z + step) % NZ, x)

    def x_device(step):
        return device(core, y, z, (x + step) % NX)

    def y_device(step):
        return device(core, (y + step) % NY, z, x)

    greet(
        pltpu.get_barrier_semaphore(),
        [ring_device(1), ring_device(NZ - 1)]
        + [x_device(step) for step in range(1, NX)]
        + [y_device(step) for step in range(1, NY)]
        + [partner],
    )

    def pair_copy(chunk):
        return send_to(
            grad.at[1 - core, :, chunk],
            cells[chunk].at[pl.ds(core * CELLS, CELLS)],
            pair_send.at[chunk],
            pair_recv.at[chunk],
            partner,
        )

    for chunk in range(CHUNKS):
        pair_copy(chunk).start()
    for chunk in range(CHUNKS):
        cells[chunk][pl.ds(core * CELLS, CELLS)] = grad[core, :, chunk]

    mix[...] = jnp.where(
        jnp.broadcast_to(tab[1:2, :], (COLUMN, ROWS)) == iota((COLUMN, ROWS), 0) + 1, 1.0, 0.0
    ).astype(BF16)

    def y_copy(chunk, step):
        return send_to(
            y_pack.at[chunk, pl.ds(((y + step) % NY) * PLACES, PLACES)],
            y_recv[chunk].at[pl.ds(y * PLACES, PLACES)],
            y_send.at[chunk, step],
            y_sem.at[chunk, step],
            y_device(step),
        )

    def x_copy(chunk, step):
        return send_to(
            x_pack.at[chunk, pl.ds(((x + step) % NX) * (PLACES * 8), PLACES * 8)],
            x_recv.at[chunk, pl.ds(x * (PLACES * 8), PLACES * 8)],
            x_send.at[chunk, step],
            x_sem.at[chunk, step],
            x_device(step),
        )

    for chunk in range(CHUNKS):
        pair_copy(chunk).wait_recv()

        def fill_y(to, carry):
            for k in range(PLACES):
                index = jnp.clip(places[0, to * PLACES + k], 0, MB * CELLS - 1)
                y_pack[chunk, to * PLACES + k] = cells[chunk][index]
            return carry

        lax.fori_loop(0, NY, fill_y, 0)
        for step in range(1, NY):
            y_copy(chunk, step).start()
        own = pl.ds(y * PLACES, PLACES)
        y_recv[chunk][own] = y_pack[chunk, own]

    def along_x(chunk):
        for step in range(1, NY):
            y_copy(chunk, step).wait_recv()

        def fill_x(to, carry):
            for k in range(PLACES):
                index = jnp.clip(places[8 + to, k], 1, ROWS) - 1
                spot = pl.ds(pl.multiple_of((to * PLACES + k) * 8, 8), 8)
                x_pack[chunk, spot] = y_recv[chunk][index]
            return carry

        lax.fori_loop(0, NX, fill_x, 0)
        for step in range(1, NX):
            x_copy(chunk, step).start()
        own = pl.ds(x * (PLACES * 8), PLACES * 8)
        x_recv[chunk, own] = x_pack[chunk, own]

    def block(zz):
        return pl.ds(((zz + 2 * NZ) % NZ) * (OWN * 8), OWN * 8)

    def ring_copy(chunk, direction, step):
        side = 0 if direction > 0 else 1
        reach = hops(chunk, direction)
        return send_to(
            total.at[chunk, block(z + direction * reach)]
            if step == 1
            else ring.at[chunk, side, step - 2],
            ring.at[chunk, side, step - 1],
            rs_send.at[chunk, side, step - 1],
            rs_recv.at[chunk, side, step - 1],
            ring_device(direction + NZ),
        )

    def sum_cells(chunk):
        for step in range(1, NX):
            x_copy(chunk, step).wait_recv()

        def add(r, carry):
            high, low = parts(x_recv[chunk, pl.ds(r, ROWS, stride=8), :])
            both = jnp.dot(
                mix[...], jnp.concatenate([high, low], axis=1), preferred_element_type=F32
            )
            total[chunk, pl.ds(r, COLUMN, stride=8), :] = both[:, :128] + both[:, 128:]
            return carry

        lax.fori_loop(0, 8, add, 0)
        for direction in (1, -1):
            ring_copy(chunk, direction, 1).start()

    def pass_on(chunk, step):
        for direction in (1, -1):
            reach = hops(chunk, direction)
            side = 0 if direction > 0 else 1
            if step <= reach:
                ring_copy(chunk, direction, step - 1).wait_recv()
                ring[chunk, side, step - 2] += total[
                    chunk, block(z + direction * (reach - step + 1))
                ]
                ring_copy(chunk, direction, step).start()

    def finish(chunk):
        value = total[chunk, block(z)]
        for direction in (1, -1):
            reach = hops(chunk, direction)
            side = 0 if direction > 0 else 1
            ring_copy(chunk, direction, reach).wait_recv()
            value = value + ring[chunk, side, reach - 1]
        out[:, chunk] = value.reshape(OWN, 8, 128)

    along_x(0)
    along_x(1)
    sum_cells(0)
    along_x(2)
    sum_cells(1)
    pass_on(0, 2)
    along_x(3)
    pass_on(1, 2)
    sum_cells(2)
    pass_on(0, 3)
    pass_on(1, 3)
    pass_on(2, 2)
    sum_cells(3)
    pass_on(0, 4)
    pass_on(1, 4)
    pass_on(2, 3)
    pass_on(3, 2)
    finish(0)
    finish(1)
    pass_on(2, 4)
    pass_on(3, 3)
    finish(2)
    pass_on(3, 4)
    finish(3)

    for chunk in range(CHUNKS):
        pair_copy(chunk).wait_send()
        for direction in (1, -1):
            for step in range(1, hops(chunk, direction) + 1):
                ring_copy(chunk, direction, step).wait_send()
        for step in range(1, NX):
            x_copy(chunk, step).wait_send()
            y_copy(chunk, step).wait_send()


def return_gradients(gradients, table):
    vmem = pl.BlockSpec(memory_space=pltpu.VMEM)
    smem = pl.BlockSpec(memory_space=pltpu.SMEM)
    tile = (8, 128)
    dma = pltpu.SemaphoreType.DMA
    return pl.pallas_call(
        return_kernel,
        out_shape=jax.ShapeDtypeStruct((OWN, CHUNKS) + tile, F32),
        in_specs=[vmem, smem, vmem],
        out_specs=vmem,
        scratch_shapes=[
            [pltpu.VMEM((MB * CELLS,) + tile, F32)] * CHUNKS,
            pltpu.VMEM((CHUNKS, ROWS) + tile, F32),
            [pltpu.VMEM((ROWS,) + tile, F32)] * CHUNKS,
            pltpu.VMEM((CHUNKS, ROWS * 8, 128), F32),
            pltpu.VMEM((CHUNKS, ROWS * 8, 128), F32),
            pltpu.VMEM((CHUNKS, COLUMN * 8, 128), F32),
            pltpu.VMEM((CHUNKS, 2, 4, OWN * 8, 128), F32),
            pltpu.VMEM((COLUMN, ROWS), BF16),
            dma((CHUNKS,)),
            dma((CHUNKS,)),
            dma((CHUNKS, NY)),
            dma((CHUNKS, NY)),
            dma((CHUNKS, NX)),
            dma((CHUNKS, NX)),
            dma((CHUNKS, 2, 4)),
            dma((CHUNKS, 2, 4)),
        ],
        compiler_params=pltpu.CompilerParams(collective_id=1, has_side_effects=True),
        name="return_gradients",
    )(gradients, table, table)


def swapped(block):
    return lax.ppermute(block, "section", [(0, 1), (1, 0)])


def full_windows(owned, send_plan, cell_slot):
    core = lax.axis_index("section")
    outbound = jnp.swapaxes(send_plan, 0, 1)
    patches = owned[jnp.maximum(outbound, 0)]
    arrived = lax.all_to_all(patches, "tile", split_axis=0, concat_axis=0, tiled=True)
    windows = []
    for batch in range(MB):
        flat = arrived[:, batch].reshape((-1, 2, PR, PW))
        picked = flat[cell_slot[batch]].reshape(W // PR, W // PW, 2, PR, PW)
        windows.append(jnp.transpose(picked, (2, 0, 3, 1, 4)).reshape(2, W, W))
    windows = jnp.stack(windows)
    passed = swapped(lax.dynamic_index_in_dim(windows, 1 - core, 0, keepdims=False))
    kept = lax.dynamic_index_in_dim(windows, core, 0, keepdims=False)
    first = core == 0
    return jnp.stack([jnp.where(first, kept, passed), jnp.where(first, passed, kept)])


def full_sums(gradients, send_plan, cell_slot):
    core = lax.axis_index("section")
    passed = swapped(lax.dynamic_index_in_dim(gradients, 1 - core, 0, keepdims=False))
    kept = lax.dynamic_index_in_dim(gradients, core, 0, keepdims=False)
    first = core == 0
    batches = [jnp.where(first, kept, passed), jnp.where(first, passed, kept)]
    slots = 2 * NX * NY * NZ
    placed = [
        jnp.zeros((slots, 2, PR, PW), F32)
        .at[cell_slot[batch]]
        .set(batches[batch])
        .reshape(slots // 2, 2, 2, PR, PW)
        for batch in range(MB)
    ]
    returned = lax.all_to_all(
        jnp.stack(placed, axis=1), "tile", split_axis=0, concat_axis=0, tiled=True
    )
    outbound = jnp.swapaxes(send_plan, 0, 1)
    target = jnp.where(outbound < 0, OWN, outbound).reshape(-1)
    sums = jax.ops.segment_sum(
        returned.reshape((-1, 2, PR, PW)), target, num_segments=OWN + 1
    )
    return sums[:OWN]


def body(dft, move, object_slices, probe_wave, intensities, send_list, cell_slot):
    owned = object_slices[0]
    send_plan = send_list[0]
    wanted = jnp.transpose(send_plan.reshape(MB, NY, NZ, NX, 2), (2, 1, 3, 0, 4))
    wanted = jnp.pad(wanted.reshape(NZ, 1, 64), ((0, 0), (0, 0), (0, 64)))
    wanted = jnp.broadcast_to(wanted, (NZ, 8, 128))
    windows, table, flag = fetch_windows(
        owned.reshape(OWN, CHUNKS, 8, 128), wanted, cell_slot.reshape(1, MB * CELLS)
    )
    crowded = flag[0, 0] > 0
    windows = lax.cond(
        crowded,
        lambda: full_windows(owned, send_plan, cell_slot),
        lambda: windows,
    )
    gradients = position_gradients(windows, probe_wave, intensities, dft, move)
    sums = lax.cond(
        crowded,
        lambda: full_sums(gradients, send_plan, cell_slot),
        lambda: return_gradients(
            gradients.reshape(2, CELLS, CHUNKS, 8, 128), table
        ).reshape(OWN, 2, PR, PW),
    )
    return sums[None]


def solution(mesh):
    dft, move = matrix_tables()
    in_specs = (
        P("section", "tile", None, None, None),
        P(),
        P("tile", None, None),
        P("tile", None, None, None),
        P("tile", None),
    )
    out_specs = P("section", "tile", None, None, None)
    step = functools.partial(body, jnp.asarray(dft), jnp.asarray(move))
    return jax.shard_map(step, mesh=mesh, in_specs=in_specs, out_specs=out_specs, check_vma=False)
```

time: 178 us -> 168 us (0.944)
  Pallas kernels: 169 us -> 161 us
    pallas_call x1, Pallas kernels: 78.5 us -> 71.6 us  [return_gradients(): pl.pallas_call(return_kernel, out_shape=jax.ShapeDtypeStruct((OWN, CHUNKS...]
where the time goes in v2:
time: 168 us
  Pallas kernels  161 us (96%)
  local copies, waits for them, and re-layouts  5.78 us (3%)
    pallas_call x1, Pallas kernels, fetch_windows(): pl.pallas_call(gather_kernel, out_shape=(jax.ShapeDtypeStruct((2, 2, W, W...  81.7 us
    pallas_call x1, Pallas kernels, return_gradients(): pl.pallas_call(return_kernel, out_shape=jax.ShapeDtypeStruct((OWN, CHUNKS...  71.6 us
    pallas_call x1, Pallas kernels, position_gradients(): pl.pallas_call(position_kernel, out_shape=jax.ShapeDtypeStruct((2, CELLS,...  7.54 us

profile of v2, /device:TPU:32, one launch (start us, length us, event | category | flops | bytes accessed | tf_op | source)
XLA Modules:
  0.0 167.5 jit_solution(15377076948598602776)
XLA Ops:
  0.0 0.8 reshape_squeeze.7
  0.8 0.2 copy.16
  1.0 0.1 copy.17
  1.0 0.6 broadcast_in_dim.26.meta
  1.7 1.3 reshape.152.cells
  3.0 81.7 %fetch_windows.1 = (f32[2,2,256,256]{3,2,1,0:T(8,128)S(1)}, s32[16,128]{1,0:T(8,128)S(1)}, s32[8,128]{1,0:T(8,128)}) custom-call(f32[32,4,8,128]{3,2,1,0:T(8,128)} %bitcast.64, s32[8,8,128]{2,1,0:T(8,128)} %broadcast_in_dim.26.meta, s32[1,64]{1,0:T(1,128)} %reshape.152.cells), custom_call_target="tpu_custom_call" | custom-call | tf_op jit(solution)/shard_map/fetch_windows/pallas_call | solution.py:468
  84.7 1.2 slice.24
  86.5 0.8 copy.18
  87.4 0.2 conditional.2
  87.6 0.0 copy-start
  87.6 7.5 %position_gradients.1 = f32[2,32,2,16,128]{4,3,2,1,0:T(8,128)S(1)} custom-call(f32[2,2,256,256]{3,2,1,0:T(8,128)S(1)} %get-tuple-element.59.win, f32[2,256,256]{2,1,0:T(8,128)} %probe.1, f32[2,256,256]{2,1,0:T(8,128)} %measured.1, bf16[512,768]{1,0:T(8,128)(2,1)} %constant.61.clone.dft, bf16[512,768]{1,0:T(8,128)(2,1)} %constant.62.clone.move), custom_call_target="tpu_custom_call" | custom-call | tf_op jit(solution)/shard_map/position_gradients/pallas_call | solution.py:572
  95.1 0.0 copy-done
  95.1 71.6 %conditional.3 = (f32[1,32,2,16,128]{4,3,2,1,0:T(8,128)S(1)}) conditional(s32[]{:T(128)} %bitcast.36, (f32[2,32,2,16,128]{4,3,2,1,0:T(8,128)S(1)}, s32[16,128]{1,0:T(8,128)S(1)}) %tuple.20, (s32[2,128,2]{2,0,1:T(2,128)S(1)}, s32[2,32]{1,0:T(2,128)S(1)}, f32[2,32,2,16,128]{4,3,2,1,0:T(8,128)S(1)}) %tuple.36), branch_computations={%region_2.3_spmd, %region_3.7_spmd} | conditional | flops 4457675 | bytes 85486560 | solution.py:873
  95.1 71.6 %return_gradients.1 = f32[32,4,8,128]{3,2,1,0:T(8,128)S(1)} custom-call(f32[2,32,4,8,128]{4,3,2,1,0:T(8,128)S(1)} %bitcast.69, s32[16,128]{1,0:T(8,128)S(1)} %get-tuple-element.34.places.tab, s32[16,128]{1,0:T(8,128)S(1)} %get-tuple-element.34.places.tab), custom_call_target="tpu_custom_call" | custom-call | tf_op jit(solution)/shard_map/cond/branch_0_fun/return_gradients/pallas_call | solution.py:783
  166.7 0.8 copy.28
  (1 shorter events, 0.0 us)
Async XLA Ops:
  87.6 7.6 %copy-start = (s32[2,32]{1,0:T(2,128)S(1)}, s32[2,32]{1,0:T(2,128)}, u32[]{:S(2)}) copy-start(s32[2,32]{1,0:T(2,128)} %param.15) | copy-start | bytes 772

commit v3 on v2

--- a/solution.py
+++ b/solution.py
@@ -20,7 +20,8 @@
 COLUMN = NZ * OWN
 PLACES = 32
 ROWS = 4 * PLACES
-CHUNKS = 4
+CHUNKS = 8
+TALL = 4
 PHASE_SCALE = 20.0
 MESH = pl.DeviceIdType.MESH
 F32 = jnp.float32
@@ -28,11 +29,157 @@
 BF16 = jnp.bfloat16
 
 
+FETCH = (
+    ("s", 0, -1, 1),
+    ("s", 0, 1, 1),
+    ("s", 1, -1, 1),
+    ("s", 1, 1, 1),
+    ("s", 2, -1, 1),
+    ("s", 2, 1, 1),
+    ("s", 0, -1, 2),
+    ("s", 0, 1, 2),
+    ("s", 1, -1, 2),
+    ("s", 1, 1, 2),
+    ("s", 2, -1, 2),
+    ("s", 2, 1, 2),
+    ("s", 0, -1, 3),
+    ("s", 0, 1, 3),
+    ("s", 1, -1, 3),
+    ("s", 1, 1, 3),
+    ("s", 2, -1, 3),
+    ("s", 2, 1, 3),
+    ("s", 0, 1, 4),
+    ("s", 3, -1, 1),
+    ("s", 1, -1, 4),
+    ("s", 3, 1, 1),
+    ("s", 2, 1, 4),
+    ("s", 4, -1, 1),
+    ("s", 3, -1, 2),
+    ("x", 0),
+    ("s", 4, 1, 1),
+    ("x", 1),
+    ("s", 3, 1, 2),
+    ("s", 5, -1, 1),
+    ("s", 4, -1, 2),
+    ("x", 2),
+    ("s", 5, 1, 1),
+    ("s", 3, -1, 3),
+    ("s", 4, 1, 2),
+    ("s", 5, -1, 2),
+    ("s", 3, 1, 3),
+    ("y", 0),
+    ("s", 4, -1, 3),
+    ("s", 5, 1, 2),
+    ("s", 3, -1, 4),
+    ("s", 4, 1, 3),
+    ("y", 1),
+    ("s", 5, -1, 3),
+    ("s", 6, 1, 1),
+    ("s", 5, 1, 3),
+    ("y", 2),
+    ("s", 6, -1, 1),
+    ("x", 3),
+    ("s", 4, 1, 4),
+    ("s", 7, -1, 1),
+    ("s", 5, -1, 4),
+    ("s", 6, 1, 2),
+    ("t", 0),
+    ("s", 6, -1, 2),
+    ("s", 7, 1, 1),
+    ("x", 4),
+    ("s", 7, -1, 2),
+    ("y", 3),
+    ("s", 6, 1, 3),
+    ("x", 5),
+    ("s", 7, 1, 2),
+    ("s", 6, -1, 3),
+    ("s", 7, -1, 3),
+    ("s", 6, 1, 4),
+    ("y", 4),
+    ("s", 7, 1, 3),
+    ("t", 1),
+    ("s", 7, -1, 4),
+    ("y", 5),
+    ("x", 6),
+    ("x", 7),
+    ("t", 2),
+    ("y", 6),
+    ("y", 7),
+    ("t", 3),
+)
+RETURN = (
+    ("x", 0),
+    ("x", 1),
+    ("a", 0),
+    ("x", 2),
+    ("a", 1),
+    ("x", 3),
+    ("p", 0, -1, 2),
+    ("p", 0, 1, 2),
+    ("x", 4),
+    ("a", 2),
+    ("p", 1, -1, 2),
+    ("p", 1, 1, 2),
+    ("p", 0, -1, 3),
+    ("p", 0, 1, 3),
+    ("x", 5),
+    ("a", 3),
+    ("p", 2, -1, 2),
+    ("p", 2, 1, 2),
+    ("x", 6),
+    ("a", 4),
+    ("p", 1, -1, 3),
+    ("p", 1, 1, 3),
+    ("p", 0, 1, 4),
+    ("x", 7),
+    ("p", 3, -1, 2),
+    ("p", 3, 1, 2),
+    ("a", 5),
+    ("p", 2, -1, 3),
+    ("p", 2, 1, 3),
+    ("p", 4, -1, 2),
+    ("p", 4, 1, 2),
+    ("a", 6),
+    ("p", 1, -1, 4),
+    ("p", 3, -1, 3),
+    ("f", 0),
+    ("a", 7),
+    ("p", 3, 1, 3),
+    ("p", 5, -1, 2),
+    ("p", 5, 1, 2),
+    ("p", 2, 1, 4),
+    ("p", 4, -1, 3),
+    ("p", 4, 1, 3),
+    ("p", 6, -1, 2),
+    ("p", 6, 1, 2),
+    ("f", 1),
+    ("p", 3, -1, 4),
+    ("p", 7, 1, 2),
+    ("p", 7, -1, 2),
+    ("p", 5, -1, 3),
+    ("p", 5, 1, 3),
+    ("f", 2),
+    ("p", 4, 1, 4),
+    ("p", 6, -1, 3),
+    ("p", 6, 1, 3),
+    ("f", 3),
+    ("p", 7, -1, 3),
+    ("p", 7, 1, 3),
+    ("p", 5, -1, 4),
+    ("f", 4),
+    ("p", 6, 1, 4),
+    ("p", 7, -1, 4),
+    ("f", 5),
+    ("f", 6),
+    ("f", 7),
+)
+
+
 def stacked_parts(matrix):
     rows = np.concatenate([matrix.real, matrix.imag], axis=0).astype(np.float32)
     high = rows.astype(ml_dtypes.bfloat16)
     low = (rows - high.astype(np.float32)).astype(ml_dtypes.bfloat16)
-    return np.concatenate([high, high, low], axis=1)
+    return np.concatenate([high, low], axis=1)
 
 
 def matrix_tables():
@@ -179,19 +326,16 @@
             ring_device(direction + NZ),
         ).wait_recv()
 
-    def start_ring(first):
-        for chunk in (first, first + 1):
-            for direction in (1, -1):
-                ring_copy(chunk, direction, 1).start()
-
-    def forward_ring(first, hop):
-        for chunk in (first, first + 1):
-            for direction in (1, -1):
-                ring_arrival(chunk, direction, hop - 1)
-                if hop <= hops(chunk, direction):
-                    ring_copy(chunk, direction, hop).start()
-
-    start_ring(0)
+    def ring_send(chunk, direction, hop):
+        if hop > 1:
+            ring_arrival(chunk, direction, hop - 1)
+        ring_copy(chunk, direction, hop).start()
+
+    first_wait = min(i for i, event in enumerate(FETCH) if event[0] != "s" or event[3] > 1)
+    first_x = min(i for i, event in enumerate(FETCH) if event[0] == "x")
+    first_y = min(i for i, event in enumerate(FETCH) if event[0] == "y")
+    for event in FETCH[:first_wait]:
+        ring_send(*event[1:])
 
     row = cells[...]
     owner = row >> 1
@@ -238,9 +382,9 @@
     for chunk in range(CHUNKS):
         ag[chunk][pl.ds(z * OWN, OWN)] = obj[:, chunk]
 
-    forward_ring(0, 2)
-    forward_ring(0, 3)
-    start_ring(2)
+    half_way = (first_wait + first_x) // 2
+    for event in FETCH[first_wait:half_way]:
+        ring_send(*event[1:])
 
     for step in range(1, NZ):
         meta_copy(step).wait()
@@ -307,9 +451,8 @@
     for part in range(PLACES // 8):
         table_copy(1 + part, pick.at[part]).wait()
 
-    forward_ring(0, 4)
-    ring_arrival(0, 1, 4)
-    ring_arrival(1, -1, 4)
+    for event in FETCH[half_way:first_x]:
+        ring_send(*event[1:])
 
     def x_copy(chunk, step):
         return send_to(
@@ -330,6 +473,9 @@
         )
 
     def along_x(chunk):
+        for direction in (1, -1):
+            ring_arrival(chunk, direction, hops(chunk, direction))
+
         def fill(to, carry):
             for k in range(PLACES):
                 index = jnp.clip(pick[k // 8, k % 8, to * 4], 1, COLUMN) - 1
@@ -367,26 +513,42 @@
             partner,
         )
 
-    def take(chunk):
-        for step in range(1, NY):
-            y_copy(chunk, step).wait_recv()
-        part, half = chunk // 2, chunk % 2
+    def take(quarter):
+        low, high = 2 * quarter, 2 * quarter + 1
+        for chunk in (low, high):
+            for step in range(1, NY):
+                y_copy(chunk, step).wait_recv()
+        part, half = quarter // 2, quarter % 2
+
+        def both(index):
+            index = jnp.clip(index, 0, ROWS - 1)
+            return jnp.concatenate([y_recv[low][index], y_recv[high][index]], axis=0)
 
         def lay(r, carry):
             first = pl.multiple_of(r * PR + half * 8, 8)
             for side in range(2):
                 k = r * 2 + side
                 lanes_of = slice(side * PW, side * PW + PW)
-                keep = jnp.clip(slot[0, core * CELLS + k], 0, ROWS - 1)
-                give = jnp.clip(slot[0, (1 - core) * CELLS + k], 0, ROWS - 1)
-                win[core, part, pl.ds(first, 8), lanes_of] = y_recv[chunk][keep]
-                other[part, pl.ds(first, 8), lanes_of] = y_recv[chunk][give]
+                win[core, part, pl.ds(first, 8), lanes_of] = both(slot[0, core * CELLS + k])
+                other[part, pl.ds(first, 8), lanes_of] = both(slot[0, (1 - core) * CELLS + k])
             return carry
 
         lax.fori_loop(0, W // PR, lay, 0)
 
-    along_x(0)
-    along_x(1)
+    def run(events):
+        for event in events:
+            if event[0] == "s":
+                ring_send(*event[1:])
+            elif event[0] == "x":
+                along_x(event[1])
+            elif event[0] == "y":
+                along_y(event[1])
+            else:
+                take(event[1])
+                if event[1] % 2 == 1:
+                    pair_copy(event[1] // 2).start()
+
+    run(FETCH[first_x:first_y])
 
     for step in range(1, NX):
         mark_copy(0, step).wait()
@@ -424,32 +586,19 @@
         mark_copy(1, step).start()
     table_copy(last, turn).wait()
 
-    forward_ring(2, 2)
-    along_y(0)
-    forward_ring(2, 3)
-    along_y(1)
+    next_y = [i for i, event in enumerate(FETCH) if event[0] == "y"]
+    run(FETCH[first_y : next_y[2]])
     for step in range(1, NY):
         mark_copy(1, step).wait()
     mark[2] = jnp.max(marks_y[...].astype(F32), axis=0).astype(I32)
     marks_z[z] = mark[2]
     for step in range(1, NZ):
         mark_copy(2, step).start()
-    forward_ring(2, 4)
-    ring_arrival(2, 1, 4)
-    along_x(2)
-    ring_arrival(3, -1, 4)
-    along_x(3)
-    take(0)
-    take(1)
-    pair_copy(0).start()
+    run(FETCH[next_y[2] : next_y[5]])
     for step in range(1, NZ):
         mark_copy(2, step).wait()
     flag[...] = jnp.max(marks_z[...].astype(F32), axis=0).astype(I32)
-    along_y(2)
-    along_y(3)
-    take(2)
-    take(3)
-    pair_copy(1).start()
+    run(FETCH[next_y[5] :])
     for chunk in range(CHUNKS):
         for direction in (1, -1):
             for hop in range(1, hops(chunk, direction) + 1):
@@ -463,7 +612,7 @@
 
 def fetch_windows(owned, wanted, cells):
     vmem = pl.BlockSpec(memory_space=pltpu.VMEM)
-    tile = (8, 128)
+    tile, strip = (8, PW), (TALL, PW)
     dma = pltpu.SemaphoreType.DMA
     return pl.pallas_call(
         gather_kernel,
@@ -475,17 +624,17 @@
         in_specs=[vmem] * 3,
         out_specs=(vmem, vmem, vmem),
         scratch_shapes=[
-            [pltpu.VMEM((COLUMN,) + tile, F32)] * CHUNKS,
+            [pltpu.VMEM((COLUMN,) + strip, F32)] * CHUNKS,
             pltpu.VMEM((NZ,) + tile, I32),
             pltpu.VMEM((NZ,) + tile, I32),
             pltpu.VMEM((2 + PLACES // 8,) + tile, I32),
             pltpu.SMEM((PLACES // 8,) + tile, I32),
             pltpu.SMEM(tile, I32),
             pltpu.SMEM(tile, I32),
-            pltpu.VMEM((CHUNKS, ROWS) + tile, F32),
-            [pltpu.VMEM((ROWS,) + tile, F32)] * CHUNKS,
-            pltpu.VMEM((CHUNKS, ROWS) + tile, F32),
-            [pltpu.VMEM((ROWS,) + tile, F32)] * CHUNKS,
+            pltpu.VMEM((CHUNKS, ROWS) + strip, F32),
+            [pltpu.VMEM((ROWS,) + strip, F32)] * CHUNKS,
+            pltpu.VMEM((CHUNKS, ROWS) + strip, F32),
+            [pltpu.VMEM((ROWS,) + strip, F32)] * CHUNKS,
             pltpu.VMEM((3,) + tile, I32),
             pltpu.VMEM((NX,) + tile, I32),
             pltpu.VMEM((NY,) + tile, I32),
@@ -518,19 +667,17 @@
 def from_left(real, imag, table, sign):
     high, low = parts(jnp.concatenate([real, imag], axis=1))
     out = jnp.dot(
-        table[...], jnp.concatenate([high, low, high], axis=0), preferred_element_type=F32
-    )
+        table[...], jnp.concatenate([high, high], axis=0), preferred_element_type=F32
+    ) + jnp.dot(table[:, :W], low, preferred_element_type=F32)
     return out[:W, :W] - sign * out[W:, W:], out[:W, W:] + sign * out[W:, :W]
 
 
 def from_right(real, imag, table, sign):
     high, low = parts(jnp.concatenate([real, imag], axis=0))
+    across = (((1,), (1,)), ((), ()))
     out = lax.dot_general(
-        jnp.concatenate([high, low, high], axis=1),
-        table[...],
-        (((1,), (1,)), ((), ())),
-        preferred_element_type=F32,
-    )
+        jnp.concatenate([high, high], axis=1), table[...], across, preferred_element_type=F32
+    ) + lax.dot_general(low, table[:, :W], across, preferred_element_type=F32)
     return out[:W, :W] - sign * out[W:, W:], sign * out[:W, W:] + out[W:, :W]
 
 
@@ -649,8 +796,8 @@
 
     def x_copy(chunk, step):
         return send_to(
-            x_pack.at[chunk, pl.ds(((x + step) % NX) * (PLACES * 8), PLACES * 8)],
-            x_recv.at[chunk, pl.ds(x * (PLACES * 8), PLACES * 8)],
+            x_pack.at[chunk, pl.ds(((x + step) % NX) * (PLACES * TALL), PLACES * TALL)],
+            x_recv.at[chunk, pl.ds(x * (PLACES * TALL), PLACES * TALL)],
             x_send.at[chunk, step],
             x_sem.at[chunk, step],
             x_device(step),
@@ -676,20 +823,20 @@
             y_copy(chunk, step).wait_recv()
 
         def fill_x(to, carry):
-            for k in range(PLACES):
-                index = jnp.clip(places[8 + to, k], 1, ROWS) - 1
-                spot = pl.ds(pl.multiple_of((to * PLACES + k) * 8, 8), 8)
-                x_pack[chunk, spot] = y_recv[chunk][index]
+            for k in range(0, PLACES, 2):
+                two = [jnp.clip(places[8 + to, k + i], 1, ROWS) - 1 for i in range(2)]
+                spot = pl.ds(pl.multiple_of((to * PLACES + k) * TALL, 8), 2 * TALL)
+                x_pack[chunk, spot] = jnp.concatenate([y_recv[chunk][i] for i in two], axis=0)
             return carry
 
         lax.fori_loop(0, NX, fill_x, 0)
         for step in range(1, NX):
             x_copy(chunk, step).start()
-        own = pl.ds(x * (PLACES * 8), PLACES * 8)
+        own = pl.ds(x * (PLACES * TALL), PLACES * TALL)
         x_recv[chunk, own] = x_pack[chunk, own]
 
     def block(zz):
-        return pl.ds(((zz + 2 * NZ) % NZ) * (OWN * 8), OWN * 8)
+        return pl.ds(((zz + 2 * NZ) % NZ) * (OWN * TALL), OWN * TALL)
 
     def ring_copy(chunk, direction, step):
         side = 0 if direction > 0 else 1
@@ -709,61 +856,52 @@
             x_copy(chunk, step).wait_recv()
 
         def add(r, carry):
-            high, low = parts(x_recv[chunk, pl.ds(r, ROWS, stride=8), :])
+            high, low = parts(x_recv[chunk, pl.ds(r, ROWS, stride=TALL), :])
             both = jnp.dot(
                 mix[...], jnp.concatenate([high, low], axis=1), preferred_element_type=F32
             )
-            total[chunk, pl.ds(r, COLUMN, stride=8), :] = both[:, :128] + both[:, 128:]
+            total[chunk, pl.ds(r, COLUMN, stride=TALL), :] = both[:, :128] + both[:, 128:]
             return carry
 
-        lax.fori_loop(0, 8, add, 0)
+        lax.fori_loop(0, TALL, add, 0)
         for direction in (1, -1):
             ring_copy(chunk, direction, 1).start()
 
-    def pass_on(chunk, step):
-        for direction in (1, -1):
-            reach = hops(chunk, direction)
-            side = 0 if direction > 0 else 1
-            if step <= reach:
-                ring_copy(chunk, direction, step - 1).wait_recv()
-                ring[chunk, side, step - 2] += total[
-                    chunk, block(z + direction * (reach - step + 1))
-                ]
-                ring_copy(chunk, direction, step).start()
-
-    def finish(chunk):
+    def pass_on(chunk, direction, step):
+        reach = hops(chunk, direction)
+        side = 0 if direction > 0 else 1
+        ring_copy(chunk, direction, step - 1).wait_recv()
+        ring[chunk, side, step - 2] += total[chunk, block(z + direction * (reach - step + 1))]
+        ring_copy(chunk, direction, step).start()
+
+    def last(chunk):
         value = total[chunk, block(z)]
         for direction in (1, -1):
             reach = hops(chunk, direction)
             side = 0 if direction > 0 else 1
             ring_copy(chunk, direction, reach).wait_recv()
             value = value + ring[chunk, side, reach - 1]
-        out[:, chunk] = value.reshape(OWN, 8, 128)
-
-    along_x(0)
-    along_x(1)
-    sum_cells(0)
-    along_x(2)
-    sum_cells(1)
-    pass_on(0, 2)
-    along_x(3)
-    pass_on(1, 2)
-    sum_cells(2)
-    pass_on(0, 3)
-    pass_on(1, 3)
-    pass_on(2, 2)
-    sum_cells(3)
-    pass_on(0, 4)
-    pass_on(1, 4)
-    pass_on(2, 3)
-    pass_on(3, 2)
-    finish(0)
-    finish(1)
-    pass_on(2, 4)
-    pass_on(3, 3)
-    finish(2)
-    pass_on(3, 4)
-    finish(3)
+        return value
+
+    def finish(quarter):
+        low, high = last(2 * quarter), last(2 * quarter + 1)
+        for p in range(OWN):
+            rows = slice(p * TALL, p * TALL + TALL)
+            spot = p * CHUNKS * TALL + quarter * 8
+            out[spot : spot + 8] = jnp.concatenate([low[rows], high[rows]], axis=0)
+
+    ended = set()
+    for event in RETURN:
+        if event[0] == "x":
+            along_x(event[1])
+        elif event[0] == "a":
+            sum_cells(event[1])
+        elif event[0] == "p":
+            pass_on(*event[1:])
+        else:
+            ended.add(event[1])
+            if event[1] ^ 1 in ended:
+                finish(event[1] // 2)
 
     for chunk in range(CHUNKS):
         pair_copy(chunk).wait_send()
@@ -778,21 +916,21 @@
 def return_gradients(gradients, table):
     vmem = pl.BlockSpec(memory_space=pltpu.VMEM)
     smem = pl.BlockSpec(memory_space=pltpu.SMEM)
-    tile = (8, 128)
+    tile, strip = (8, PW), (TALL, PW)
     dma = pltpu.SemaphoreType.DMA
     return pl.pallas_call(
         return_kernel,
-        out_shape=jax.ShapeDtypeStruct((OWN, CHUNKS) + tile, F32),
+        out_shape=jax.ShapeDtypeStruct((OWN * CHUNKS * TALL, PW), F32),
         in_specs=[vmem, smem, vmem],
         out_specs=vmem,
         scratch_shapes=[
-            [pltpu.VMEM((MB * CELLS,) + tile, F32)] * CHUNKS,
-            pltpu.VMEM((CHUNKS, ROWS) + tile, F32),
-            [pltpu.VMEM((ROWS,) + tile, F32)] * CHUNKS,
-            pltpu.VMEM((CHUNKS, ROWS * 8, 128), F32),
-            pltpu.VMEM((CHUNKS, ROWS * 8, 128), F32),
-            pltpu.VMEM((CHUNKS, COLUMN * 8, 128), F32),
-            pltpu.VMEM((CHUNKS, 2, 4, OWN * 8, 128), F32),
+            [pltpu.VMEM((MB * CELLS,) + strip, F32)] * CHUNKS,
+            pltpu.VMEM((CHUNKS, ROWS) + strip, F32),
+            [pltpu.VMEM((ROWS,) + strip, F32)] * CHUNKS,
+            pltpu.VMEM((CHUNKS, ROWS * TALL, 128), F32),
+            pltpu.VMEM((CHUNKS, ROWS * TALL, 128), F32),
+            pltpu.VMEM((CHUNKS, COLUMN * TALL, 128), F32),
+            pltpu.VMEM((CHUNKS, 2, 4, OWN * TALL, 128), F32),
             pltpu.VMEM((COLUMN, ROWS), BF16),
             dma((CHUNKS,)),
             dma((CHUNKS,)),
@@ -861,7 +999,7 @@
     wanted = jnp.pad(wanted.reshape(NZ, 1, 64), ((0, 0), (0, 0), (0, 64)))
     wanted = jnp.broadcast_to(wanted, (NZ, 8, 128))
     windows, table, flag = fetch_windows(
-        owned.reshape(OWN, CHUNKS, 8, 128), wanted, cell_slot.reshape(1, MB * CELLS)
+        owned.reshape(OWN, CHUNKS, TALL, PW), wanted, cell_slot.reshape(1, MB * CELLS)
     )
     crowded = flag[0, 0] > 0
     windows = lax.cond(
@@ -874,7 +1012,7 @@
         crowded,
         lambda: full_sums(gradients, send_plan, cell_slot),
         lambda: return_gradients(
-            gradients.reshape(2, CELLS, CHUNKS, 8, 128), table
+            gradients.reshape(2, CELLS, CHUNKS, TALL, PW), table
         ).reshape(OWN, 2, PR, PW),
     )
     return sums[None]

time: 168 us -> 151 us (0.90)
  Pallas kernels: 161 us -> 144 us
    pallas_call x1, Pallas kernels: 81.7 us -> 72.7 us  [fetch_windows(): pl.pallas_call(gather_kernel, out_shape=(jax.ShapeDtypeStruct((2, 2, W, W...]
    pallas_call x1, Pallas kernels: 71.6 us -> 63.6 us  [return_gradients(): pl.pallas_call(return_kernel, out_shape=jax.ShapeDtypeStruct((OWN * CHUNK...]
where the time goes in v3:
time: 151 us; the launch traced here: 150 us
  Pallas kernels  144 us (95%)
  local copies, waits for them, and re-layouts  5.78 us (4%)
    pallas_call x1, Pallas kernels, fetch_windows(): pl.pallas_call(gather_kernel, out_shape=(jax.ShapeDtypeStruct((2, 2, W, W...  72.7 us
    pallas_call x1, Pallas kernels, return_gradients(): pl.pallas_call(return_kernel, out_shape=jax.ShapeDtypeStruct((OWN * CHUNK...  63.6 us
    pallas_call x1, Pallas kernels, position_gradients(): pl.pallas_call(position_kernel, out_shape=jax.ShapeDtypeStruct((2, CELLS,...  7.48 us

profile of v3, /device:TPU:32, one launch (start us, length us, event | category | flops | bytes accessed | tf_op | source)
XLA Modules:
  0.0 150.4 jit_solution(14917656987816456208)
XLA Ops:
  0.0 0.8 reshape_squeeze.7
  0.8 0.2 copy.16
  1.0 0.1 copy.17
  1.0 0.6 broadcast_in_dim.26.meta
  1.7 1.3 reshape.152.cells
  3.0 72.7 %fetch_windows.1 = (f32[2,2,256,256]{3,2,1,0:T(8,128)S(1)}, s32[16,128]{1,0:T(8,128)S(1)}, s32[8,128]{1,0:T(8,128)}) custom-call(f32[32,8,4,128]{3,2,1,0:T(4,128)} %bitcast.64, s32[8,8,128]{2,1,0:T(8,128)} %broadcast_in_dim.26.meta, s32[1,64]{1,0:T(1,128)} %reshape.152.cells), custom_call_target="tpu_custom_call" | custom-call | tf_op jit(solution)/shard_map/fetch_windows/pallas_call | solution.py:617
  75.6 1.2 slice.24
  77.5 0.8 copy.18
  78.3 0.2 conditional.2
  78.5 0.0 copy-start
  78.5 7.5 %position_gradients.1 = f32[2,32,2,16,128]{4,3,2,1,0:T(8,128)S(1)} custom-call(f32[2,2,256,256]{3,2,1,0:T(8,128)S(1)} %get-tuple-element.59.win, f32[2,256,256]{2,1,0:T(8,128)} %probe.1, f32[2,256,256]{2,1,0:T(8,128)} %measured.1, bf16[512,512]{1,0:T(8,128)(2,1)} %constant.61.clone.dft, bf16[512,512]{1,0:T(8,128)(2,1)} %constant.62.clone.move), custom_call_target="tpu_custom_call" | custom-call | tf_op jit(solution)/shard_map/position_gradients/pallas_call | solution.py:719
  86.0 0.0 copy-done
  86.0 63.6 %conditional.3 = (f32[1,32,2,16,128]{4,3,2,1,0:T(8,128)S(1)}) conditional(s32[]{:T(128)} %bitcast.36, (f32[2,32,2,16,128]{4,3,2,1,0:T(8,128)S(1)}, s32[16,128]{1,0:T(8,128)S(1)}) %tuple.20, (s32[2,128,2]{2,0,1:T(2,128)S(1)}, s32[2,32]{1,0:T(2,128)S(1)}, f32[2,32,2,16,128]{4,3,2,1,0:T(8,128)S(1)}) %tuple.36), branch_computations={%region_2.3_spmd, %region_3.7_spmd} | conditional | flops 4457675 | bytes 85486560 | solution.py:1011
  86.0 63.6 %return_gradients.1 = f32[1024,128]{1,0:T(8,128)S(1)} custom-call(f32[2,32,8,4,128]{4,3,2,1,0:T(4,128)S(1)} %bitcast.69, s32[16,128]{1,0:T(8,128)S(1)} %get-tuple-element.34.places.tab, s32[16,128]{1,0:T(8,128)S(1)} %get-tuple-element.34.places.tab), custom_call_target="tpu_custom_call" | custom-call | tf_op jit(solution)/shard_map/cond/branch_0_fun/return_gradients/pallas_call | solution.py:921
  149.6 0.8 copy.28
  (1 shorter events, 0.0 us)
Async XLA Ops:
  78.5 7.5 %copy-start = (s32[2,32]{1,0:T(2,128)S(1)}, s32[2,32]{1,0:T(2,128)}, u32[]{:S(2)}) copy-start(s32[2,32]{1,0:T(2,128)} %param.15) | copy-start | bytes 772

commit v4 on v3

--- a/solution.py
+++ b/solution.py
@@ -244,7 +244,16 @@
     return 4 if (chunk % 2 == 0) == (direction > 0) else 3
 
 
-def gather_kernel(
+def fill_rows(count, move):
+    def some(part, carry):
+        for k in range(8):
+            move(part * 8 + k)
+        return carry
+
+    lax.fori_loop(0, count // 8, some, 0)
+
+
+def fetch(
     obj,
     meta,
     cells,
@@ -257,7 +266,9 @@
     tables,
     pick,
     turn,
+    turned,
     slot,
+    places,
     x_pack,
     x_recv,
     y_pack,
@@ -280,6 +291,7 @@
     pair_send,
     pair_recv,
     local_sem,
+    loads,
 ):
     core, y, z, x = place()
     partner = device(1 - core, y, z, x)
@@ -337,7 +349,10 @@
     for event in FETCH[:first_wait]:
         ring_send(*event[1:])
 
-    row = cells[...]
+    for load in loads:
+        load.start()
+
+    row = jnp.concatenate([cells[0:1, :], cells[1:2, :]], axis=1)
     owner = row >> 1
     entry = ((owner >> 2) & 7) * 4 + (iota(row.shape, 1) >> 5) * 2 + (row & 1)
     code_row = ((owner >> 5) * 128 + (owner & 3) * 32 + entry).astype(F32)
@@ -357,14 +372,14 @@
     number = iota((MB * CELLS, ROWS), 0).astype(F32)
     back_row = jnp.sum(jnp.where(spread, number, 0.0), axis=0, keepdims=True)
 
-    lane = iota((8, 128), 1)
-    for zz in range(NZ):
-        metas[zz] = jnp.where(lane == 64, jnp.broadcast_to(over, (8, 128)), meta[zz])
-    metain[z] = metas[z]
+    metas[...] = jnp.concatenate(
+        [meta[...], jnp.broadcast_to(over, (1, 128)), jnp.zeros((3, 128), I32)], axis=0
+    )
+    metain[z] = metas[...]
 
     def meta_copy(step):
         return send_to(
-            metas.at[(z + step) % NZ],
+            metas,
             metain.at[z],
             meta_send.at[step],
             meta_recv.at[step],
@@ -374,8 +389,11 @@
     for step in range(1, NZ):
         meta_copy(step).start()
 
+    last = 1 + PLACES // 8
+
     def table_copy(index, target):
-        return pltpu.make_async_copy(tables.at[index], target, local_sem.at[index])
+        source = tab if index > last else tables.at[index]
+        return pltpu.make_async_copy(source, target, local_sem.at[index])
 
     table_copy(0, slot).start()
 
@@ -388,26 +406,21 @@
 
     for step in range(1, NZ):
         meta_copy(step).wait()
-    wanted = metain[:, 0, :].astype(F32)
-    lanes = iota((NZ, 128), 1)
-    valid = (wanted >= 0.0) & (lanes < 64)
+    wanted = jnp.concatenate([metain[zz][0:4] for zz in range(NZ)], axis=0).astype(F32)
+    lanes = iota((4 * NZ, 128), 1)
+    valid = (wanted >= 0.0) & (((lanes >> 2) & 7) == z)
     held = jnp.where(valid, 1.0, 0.0)
     big_row, big_lane = iota((128, 128), 0), iota((128, 128), 1)
-    one_device = (big_row >> 2) == (big_lane >> 2)
-    one_x = ((big_row >> 2) & 3) == ((big_lane >> 2) & 3)
-    group = jnp.where(one_device, 1.0, 0.0)
-    before = jnp.where(one_device & (big_row < big_lane), 1.0, 0.0)
-    column = jnp.where(one_x & (big_row < 64), 1.0, 0.0)
-    above = jnp.where(one_x & ((big_row >> 4) < (big_lane >> 4)), 1.0, 0.0)
-    in_group = jnp.dot(held, group, preferred_element_type=F32)
-    order = jnp.dot(held, before, preferred_element_type=F32) + exclusive(in_group)
-    in_all = jnp.sum(held, axis=0, keepdims=True)
-    sums = jnp.concatenate([in_all, jnp.zeros((7, 128), F32)], axis=0)
-    count = jnp.dot(sums, group, preferred_element_type=F32)[0:1]
+    one_x = (big_row & 31) == (big_lane & 31)
+    column = jnp.where(one_x, 1.0, 0.0)
+    above = jnp.where(one_x & ((big_row >> 5) < (big_lane >> 5)), 1.0, 0.0)
+    earlier = jnp.where(iota((4 * NZ, 4 * NZ), 1) < iota((4 * NZ, 4 * NZ), 0), 1.0, 0.0)
+    count = jnp.sum(held, axis=0, keepdims=True)
+    sums = jnp.concatenate([count, jnp.zeros((7, 128), F32)], axis=0)
     start = jnp.dot(sums, above, preferred_element_type=F32)[0:1]
     whole = jnp.dot(sums, column, preferred_element_type=F32)[0:1]
-    order = order + start
-    named = iota((NZ, 128), 0).astype(F32) * OWN + wanted + 1.0
+    order = jnp.dot(earlier, held, preferred_element_type=F32) + start
+    named = (iota((4 * NZ, 128), 0) >> 2).astype(F32) * OWN + wanted + 1.0
     picks = [
         jnp.sum(jnp.where(valid & (order == float(k)), named, 0.0), axis=0, keepdims=True)
         for k in range(PLACES)
@@ -418,7 +431,7 @@
         table_copy(1 + part, pick.at[part]).start()
     over_x = jnp.where(jnp.max(whole, axis=1, keepdims=True) > PLACES, 1.0, 0.0)
     over_z = jnp.max(
-        jnp.max(jnp.where(lanes == 64, wanted, 0.0), axis=1, keepdims=True), axis=0, keepdims=True
+        jnp.max(metain[:, 4, :].astype(F32), axis=1, keepdims=True), axis=0, keepdims=True
     )
     over = jnp.broadcast_to(jnp.maximum(over_x, over_z), (1, 128))
     mark[0] = jnp.concatenate([count, start, over, jnp.zeros((5, 128), F32)], axis=0).astype(I32)
@@ -439,7 +452,7 @@
     for step in range(1, NX):
         mark_copy(0, step).start()
     target = iota((128, ROWS), 1)
-    chosen = jnp.where(iota((128, ROWS), 0) == (target // PLACES) * 4, 1.0, 0.0)
+    chosen = jnp.where(iota((128, ROWS), 0) == (target // PLACES) + z * 4, 1.0, 0.0)
     chosen = jnp.dot(picks, chosen, preferred_element_type=F32)
     here = iota((PLACES, ROWS), 0) == iota((PLACES, ROWS), 1) % PLACES
     sums_row = jnp.sum(jnp.where(here, chosen, 0.0), axis=0, keepdims=True)
@@ -476,13 +489,14 @@
         for direction in (1, -1):
             ring_arrival(chunk, direction, hops(chunk, direction))
 
-        def fill(to, carry):
-            for k in range(PLACES):
-                index = jnp.clip(pick[k // 8, k % 8, to * 4], 1, COLUMN) - 1
-                x_pack[chunk, to * PLACES + k] = ag[chunk][index]
+        def fill(part, carry):
+            for k in range(8):
+                for to in range(NX):
+                    index = jnp.clip(pick[part, k, z * 4 + to], 1, COLUMN) - 1
+                    x_pack[chunk, to * PLACES + part * 8 + k] = ag[chunk][index]
             return carry
 
-        lax.fori_loop(0, NX, fill, 0)
+        lax.fori_loop(0, PLACES // 8, fill, 0)
         for step in range(1, NX):
             x_copy(chunk, step).start()
         own = pl.ds(x * PLACES, PLACES)
@@ -492,13 +506,14 @@
         for step in range(1, NX):
             x_copy(chunk, step).wait_recv()
 
-        def fill(to, carry):
-            for k in range(PLACES):
-                index = jnp.clip(turn[to, k], 1, ROWS) - 1
-                y_pack[chunk, to * PLACES + k] = x_recv[chunk][index]
+        def fill(part, carry):
+            for k in range(8):
+                for to in range(NY):
+                    index = jnp.clip(turn[to, part * 8 + k], 1, ROWS) - 1
+                    y_pack[chunk, to * PLACES + part * 8 + k] = x_recv[chunk][index]
             return carry
 
-        lax.fori_loop(0, NY, fill, 0)
+        lax.fori_loop(0, PLACES // 8, fill, 0)
         for step in range(1, NY):
             y_copy(chunk, step).start()
         own = pl.ds(y * PLACES, PLACES)
@@ -560,7 +575,7 @@
     onward = []
     back = jnp.zeros((NX, 128), F32)
     for to in range(NY):
-        mine = four == to * 16 + x * 4
+        mine = four == to * 32 + z * 4 + x
         many = jnp.sum(jnp.where(mine, counts, 0.0), axis=1, keepdims=True)
         low = jnp.sum(jnp.where(mine, starts, 0.0), axis=1, keepdims=True)
         first = exclusive(many)
@@ -574,10 +589,10 @@
         )
         inside = (wide >= low) & (wide < low + many)
         back = back + jnp.where(inside, to * PLACES + first + wide - low + 1.0, 0.0)
-    last = 1 + PLACES // 8
     tables[last] = jnp.concatenate(onward + [jnp.zeros((4, 128), F32)], axis=0).astype(I32)
     table_copy(last, turn).start()
     tab[8:12, :] = back.astype(I32)
+    table_copy(last + 1, places).start()
     mark[1] = jnp.broadcast_to(
         jnp.max(marks_x[:, 2, :].astype(F32), axis=0, keepdims=True), (8, 128)
     ).astype(I32)
@@ -585,6 +600,7 @@
     for step in range(1, NY):
         mark_copy(1, step).start()
     table_copy(last, turn).wait()
+    table_copy(last + 1, places).wait()
 
     next_y = [i for i, event in enumerate(FETCH) if event[0] == "y"]
     run(FETCH[first_y : next_y[2]])
@@ -597,7 +613,9 @@
     run(FETCH[next_y[2] : next_y[5]])
     for step in range(1, NZ):
         mark_copy(2, step).wait()
-    flag[...] = jnp.max(marks_z[...].astype(F32), axis=0).astype(I32)
+    mark[0] = jnp.max(marks_z[...].astype(F32), axis=0).astype(I32)
+    crowded = pltpu.make_async_copy(mark.at[0], turned, local_sem.at[0])
+    crowded.start()
     run(FETCH[next_y[5] :])
     for chunk in range(CHUNKS):
         for direction in (1, -1):
@@ -606,57 +624,10 @@
         for step in range(1, NX):
             x_copy(chunk, step).wait_send()
             y_copy(chunk, step).wait_send()
+    crowded.wait()
+    flag[0, 0] = turned[0, 0]
     pair_copy(0).wait()
     pair_copy(1).wait()
-
-
-def fetch_windows(owned, wanted, cells):
-    vmem = pl.BlockSpec(memory_space=pltpu.VMEM)
-    tile, strip = (8, PW), (TALL, PW)
-    dma = pltpu.SemaphoreType.DMA
-    return pl.pallas_call(
-        gather_kernel,
-        out_shape=(
-            jax.ShapeDtypeStruct((2, 2, W, W), F32),
-            jax.ShapeDtypeStruct((16, 128), I32),
-            jax.ShapeDtypeStruct(tile, I32),
-        ),
-        in_specs=[vmem] * 3,
-        out_specs=(vmem, vmem, vmem),
-        scratch_shapes=[
-            [pltpu.VMEM((COLUMN,) + strip, F32)] * CHUNKS,
-            pltpu.VMEM((NZ,) + tile, I32),
-            pltpu.VMEM((NZ,) + tile, I32),
-            pltpu.VMEM((2 + PLACES // 8,) + tile, I32),
-            pltpu.SMEM((PLACES // 8,) + tile, I32),
-            pltpu.SMEM(tile, I32),
-            pltpu.SMEM(tile, I32),
-            pltpu.VMEM((CHUNKS, ROWS) + strip, F32),
-            [pltpu.VMEM((ROWS,) + strip, F32)] * CHUNKS,
-            pltpu.VMEM((CHUNKS, ROWS) + strip, F32),
-            [pltpu.VMEM((ROWS,) + strip, F32)] * CHUNKS,
-            pltpu.VMEM((3,) + tile, I32),
-            pltpu.VMEM((NX,) + tile, I32),
-            pltpu.VMEM((NY,) + tile, I32),
-            pltpu.VMEM((NZ,) + tile, I32),
-            pltpu.VMEM((2, W, W), F32),
-            dma((CHUNKS, 2, 4)),
-            dma((CHUNKS, 2, 4)),
-            dma((NZ,)),
-            dma((NZ,)),
-            dma((3, NZ)),
-            dma((3, NZ)),
-            dma((CHUNKS, NX)),
-            dma((CHUNKS, NX)),
-            dma((CHUNKS, NY)),
-            dma((CHUNKS, NY)),
-            dma((2,)),
-            dma((2,)),
-            dma((2 + PLACES // 8,)),
-        ],
-        compiler_params=pltpu.CompilerParams(collective_id=0, has_side_effects=True),
-        name="fetch_windows",
-    )(owned, wanted, cells)
 
 
 def parts(value):
@@ -686,16 +657,7 @@
     return from_right(real, imag, table, sign)
 
 
-def position_kernel(win, probe, measured, dft, move, grad):
-    core = lax.axis_index("section")
-
-    def lay(index, real, imag):
-        for k in range(CELLS):
-            rows = slice(k // 2 * PR, k // 2 * PR + PR)
-            lanes = slice(k % 2 * PW, k % 2 * PW + PW)
-            grad[index, k, 0] = real[rows, lanes]
-            grad[index, k, 1] = imag[rows, lanes]
-
+def position(win, probe, measured, dft, move, lay):
     pr, pi = probe[0], probe[1]
     ar, ai = win[0, 0], win[0, 1]
     wave_r, wave_i = both_sides(pr * ar - pi * ai, pr * ai + pi * ar, move, 1.0)
@@ -703,7 +665,7 @@
     far_r, far_i = both_sides(
         wave_r * br - wave_i * bi, wave_r * bi + wave_i * br, dft, 1.0
     )
-    gap = far_r * far_r + far_i * far_i - measured[core]
+    gap = far_r * far_r + far_i * far_i - measured[...]
     back_r, back_i = both_sides(gap * far_r, gap * far_i, dft, -1.0)
     lay(1, wave_r * back_r + wave_i * back_i, wave_r * back_i - wave_i * back_r)
     br, bi = win[1, 0], win[1, 1]
@@ -714,18 +676,36 @@
     lay(0, pr * low_r + pi * low_i, pr * low_i - pi * low_r)
 
 
+def lay_cells(grad):
+    def lay(index, real, imag):
+        for k in range(CELLS):
+            rows = slice(k // 2 * PR, k // 2 * PR + PR)
+            lanes = slice(k % 2 * PW, k % 2 * PW + PW)
+            for part, value in enumerate((real, imag)):
+                value = value[rows, lanes]
+                for strip in range(4):
+                    grad[index, k, part * 4 + strip] = value[strip * TALL : strip * TALL + TALL]
+
+    return lay
+
+
+def position_kernel(win, probe, measured, dft, move, grad):
+    core = lax.axis_index("section")
+    position(win, probe, measured.at[core], dft, move, lay_cells(grad))
+
+
 def position_gradients(windows, probe_wave, intensities, dft, move):
     vmem = pl.BlockSpec(memory_space=pltpu.VMEM)
     return pl.pallas_call(
         position_kernel,
-        out_shape=jax.ShapeDtypeStruct((2, CELLS, 2, PR, PW), F32),
+        out_shape=jax.ShapeDtypeStruct((2, CELLS, CHUNKS, TALL, PW), F32),
         in_specs=[vmem] * 5,
         out_specs=vmem,
         name="position_gradients",
     )(windows, probe_wave, intensities, dft, move)
 
 
-def return_kernel(
+def give_back(
     grad,
     places,
     tab,
@@ -759,14 +739,6 @@
     def y_device(step):
         return device(core, (y + step) % NY, z, x)
 
-    greet(
-        pltpu.get_barrier_semaphore(),
-        [ring_device(1), ring_device(NZ - 1)]
-        + [x_device(step) for step in range(1, NX)]
-        + [y_device(step) for step in range(1, NY)]
-        + [partner],
-    )
-
     def pair_copy(chunk):
         return send_to(
             grad.at[1 - core, :, chunk],
@@ -777,9 +749,9 @@
         )
 
     for chunk in range(CHUNKS):
+        cells[chunk][pl.ds(core * CELLS, CELLS)] = grad[core, :, chunk]
+    for chunk in range(CHUNKS):
         pair_copy(chunk).start()
-    for chunk in range(CHUNKS):
-        cells[chunk][pl.ds(core * CELLS, CELLS)] = grad[core, :, chunk]
 
     mix[...] = jnp.where(
         jnp.broadcast_to(tab[1:2, :], (COLUMN, ROWS)) == iota((COLUMN, ROWS), 0) + 1, 1.0, 0.0
@@ -806,13 +778,11 @@
     for chunk in range(CHUNKS):
         pair_copy(chunk).wait_recv()
 
-        def fill_y(to, carry):
-            for k in range(PLACES):
-                index = jnp.clip(places[0, to * PLACES + k], 0, MB * CELLS - 1)
-                y_pack[chunk, to * PLACES + k] = cells[chunk][index]
-            return carry
-
-        lax.fori_loop(0, NY, fill_y, 0)
+        def fill_y(row):
+            index = jnp.clip(places[0, row], 0, MB * CELLS - 1)
+            y_pack[chunk, row] = cells[chunk][index]
+
+        fill_rows(ROWS, fill_y)
         for step in range(1, NY):
             y_copy(chunk, step).start()
         own = pl.ds(y * PLACES, PLACES)
@@ -822,14 +792,13 @@
         for step in range(1, NY):
             y_copy(chunk, step).wait_recv()
 
-        def fill_x(to, carry):
-            for k in range(0, PLACES, 2):
-                two = [jnp.clip(places[8 + to, k + i], 1, ROWS) - 1 for i in range(2)]
-                spot = pl.ds(pl.multiple_of((to * PLACES + k) * TALL, 8), 2 * TALL)
-                x_pack[chunk, spot] = jnp.concatenate([y_recv[chunk][i] for i in two], axis=0)
-            return carry
-
-        lax.fori_loop(0, NX, fill_x, 0)
+        def fill_x(pair):
+            to, k = pair // (PLACES // 2), pair % (PLACES // 2) * 2
+            two = [jnp.clip(places[8 + to, k + i], 1, ROWS) - 1 for i in range(2)]
+            spot = pl.ds(pl.multiple_of(pair * 2 * TALL, 8), 2 * TALL)
+            x_pack[chunk, spot] = jnp.concatenate([y_recv[chunk][i] for i in two], axis=0)
+
+        fill_rows(ROWS // 2, fill_x)
         for step in range(1, NX):
             x_copy(chunk, step).start()
         own = pl.ds(x * (PLACES * TALL), PLACES * TALL)
@@ -913,41 +882,119 @@
             y_copy(chunk, step).wait_send()
 
 
-def return_gradients(gradients, table):
+def whole_kernel(obj, meta, cells, probe, measured, dft, move, out, flag, *scratch):
+    fetching, giving, (grad, probe_in, measured_in, dft_in, move_in, load_sem) = scratch
+    win, tab, places = fetching["win"], fetching["tab"], fetching["places"]
+    core = lax.axis_index("section")
+    loads = [
+        pltpu.make_async_copy(source, target, load_sem.at[index])
+        for index, (source, target) in enumerate(
+            (
+                (probe, probe_in),
+                (measured.at[core], measured_in),
+                (dft, dft_in),
+                (move, move_in),
+            )
+        )
+    ]
+    fetch(obj, meta, cells, flag=flag, loads=loads, **fetching)
+    for load in loads:
+        load.wait()
+    position(win, probe_in, measured_in, dft_in, move_in, lay_cells(grad))
+    del win
+    give_back(grad, places, tab, out, **giving)
+
+
+def object_sums(owned, meta, cells, probe_wave, intensities, dft, move):
     vmem = pl.BlockSpec(memory_space=pltpu.VMEM)
-    smem = pl.BlockSpec(memory_space=pltpu.SMEM)
+    anywhere = pl.BlockSpec(memory_space=pltpu.HBM)
     tile, strip = (8, PW), (TALL, PW)
     dma = pltpu.SemaphoreType.DMA
+    many, one = pltpu.VMEM((CHUNKS, ROWS) + strip, F32), pltpu.VMEM((ROWS,) + strip, F32)
+    fetching = dict(
+        win=pltpu.VMEM((2, 2, W, W), F32),
+        tab=pltpu.VMEM((16, 128), I32),
+        ag=[pltpu.VMEM((COLUMN,) + strip, F32)] * CHUNKS,
+        metas=pltpu.VMEM(tile, I32),
+        metain=pltpu.VMEM((NZ,) + tile, I32),
+        tables=pltpu.VMEM((2 + PLACES // 8,) + tile, I32),
+        pick=pltpu.SMEM((PLACES // 8,) + tile, I32),
+        turn=pltpu.SMEM(tile, I32),
+        turned=pltpu.SMEM(tile, I32),
+        slot=pltpu.SMEM(tile, I32),
+        places=pltpu.SMEM((16, 128), I32),
+        x_pack=many,
+        x_recv=[one] * CHUNKS,
+        y_pack=many,
+        y_recv=[one] * CHUNKS,
+        mark=pltpu.VMEM((3,) + tile, I32),
+        marks_x=pltpu.VMEM((NX,) + tile, I32),
+        marks_y=pltpu.VMEM((NY,) + tile, I32),
+        marks_z=pltpu.VMEM((NZ,) + tile, I32),
+        other=pltpu.VMEM((2, W, W), F32),
+        ag_send=dma((CHUNKS, 2, 4)),
+        ag_recv=dma((CHUNKS, 2, 4)),
+        meta_send=dma((NZ,)),
+        meta_recv=dma((NZ,)),
+        mark_send=dma((3, NZ)),
+        mark_recv=dma((3, NZ)),
+        x_send=dma((CHUNKS, NX)),
+        x_sem=dma((CHUNKS, NX)),
+        y_send=dma((CHUNKS, NY)),
+        y_sem=dma((CHUNKS, NY)),
+        pair_send=dma((2,)),
+        pair_recv=dma((2,)),
+        local_sem=dma((3 + PLACES // 8,)),
+    )
+    giving = dict(
+        cells=[pltpu.VMEM((MB * CELLS,) + strip, F32)] * CHUNKS,
+        y_pack=many,
+        y_recv=[one] * CHUNKS,
+        x_pack=pltpu.VMEM((CHUNKS, ROWS * TALL, PW), F32),
+        x_recv=pltpu.VMEM((CHUNKS, ROWS * TALL, PW), F32),
+        total=pltpu.VMEM((CHUNKS, COLUMN * TALL, PW), F32),
+        ring=pltpu.VMEM((CHUNKS, 2, 4, OWN * TALL, PW), F32),
+        mix=pltpu.VMEM((COLUMN, ROWS), BF16),
+        pair_send=dma((CHUNKS,)),
+        pair_recv=dma((CHUNKS,)),
+        y_send=dma((CHUNKS, NY)),
+        y_sem=dma((CHUNKS, NY)),
+        x_send=dma((CHUNKS, NX)),
+        x_sem=dma((CHUNKS, NX)),
+        rs_send=dma((CHUNKS, 2, 4)),
+        rs_recv=dma((CHUNKS, 2, 4)),
+    )
+    rest = [
+        pltpu.VMEM((2, CELLS, CHUNKS) + strip, F32),
+        pltpu.VMEM((2, W, W), F32),
+        pltpu.VMEM((W, W), F32),
+        pltpu.VMEM((2 * W, 2 * W), BF16),
+        pltpu.VMEM((2 * W, 2 * W), BF16),
+        dma((4,)),
+    ]
     return pl.pallas_call(
-        return_kernel,
-        out_shape=jax.ShapeDtypeStruct((OWN * CHUNKS * TALL, PW), F32),
-        in_specs=[vmem, smem, vmem],
-        out_specs=vmem,
-        scratch_shapes=[
-            [pltpu.VMEM((MB * CELLS,) + strip, F32)] * CHUNKS,
-            pltpu.VMEM((CHUNKS, ROWS) + strip, F32),
-            [pltpu.VMEM((ROWS,) + strip, F32)] * CHUNKS,
-            pltpu.VMEM((CHUNKS, ROWS * TALL, 128), F32),
-            pltpu.VMEM((CHUNKS, ROWS * TALL, 128), F32),
-            pltpu.VMEM((CHUNKS, COLUMN * TALL, 128), F32),
-            pltpu.VMEM((CHUNKS, 2, 4, OWN * TALL, 128), F32),
-            pltpu.VMEM((COLUMN, ROWS), BF16),
-            dma((CHUNKS,)),
-            dma((CHUNKS,)),
-            dma((CHUNKS, NY)),
-            dma((CHUNKS, NY)),
-            dma((CHUNKS, NX)),
-            dma((CHUNKS, NX)),
-            dma((CHUNKS, 2, 4)),
-            dma((CHUNKS, 2, 4)),
-        ],
-        compiler_params=pltpu.CompilerParams(collective_id=1, has_side_effects=True),
-        name="return_gradients",
-    )(gradients, table, table)
+        whole_kernel,
+        out_shape=(
+            jax.ShapeDtypeStruct((OWN * CHUNKS * TALL, PW), F32),
+            jax.ShapeDtypeStruct((1, 1), I32),
+        ),
+        in_specs=[vmem] * 3 + [anywhere] * 4,
+        out_specs=(vmem, pl.BlockSpec(memory_space=pltpu.SMEM)),
+        scratch_shapes=[fetching, giving, rest],
+        compiler_params=pltpu.CompilerParams(
+            collective_id=0, has_side_effects=True, vmem_limit_bytes=46 << 20
+        ),
+        name="object_sums",
+    )(owned, meta, cells, probe_wave, intensities, dft, move)
 
 
 def swapped(block):
     return lax.ppermute(block, "section", [(0, 1), (1, 0)])
+
+
+def place_in_all(cell_slot):
+    batch = iota(cell_slot.shape, 0)
+    return ((cell_slot >> 1) * (2 * MB) + batch * 2 + (cell_slot & 1)).reshape(-1)
 
 
 def full_windows(owned, send_plan, cell_slot):
@@ -955,12 +1002,9 @@
     outbound = jnp.swapaxes(send_plan, 0, 1)
     patches = owned[jnp.maximum(outbound, 0)]
     arrived = lax.all_to_all(patches, "tile", split_axis=0, concat_axis=0, tiled=True)
-    windows = []
-    for batch in range(MB):
-        flat = arrived[:, batch].reshape((-1, 2, PR, PW))
-        picked = flat[cell_slot[batch]].reshape(W // PR, W // PW, 2, PR, PW)
-        windows.append(jnp.transpose(picked, (2, 0, 3, 1, 4)).reshape(2, W, W))
-    windows = jnp.stack(windows)
+    picked = arrived.reshape((-1, 2, PR, PW))[place_in_all(cell_slot)]
+    picked = picked.reshape(MB, W // PR, W // PW, 2, PR, PW)
+    windows = jnp.transpose(picked, (0, 3, 1, 4, 2, 5)).reshape(MB, 2, W, W)
     passed = swapped(lax.dynamic_index_in_dim(windows, 1 - core, 0, keepdims=False))
     kept = lax.dynamic_index_in_dim(windows, core, 0, keepdims=False)
     first = core == 0
@@ -972,17 +1016,15 @@
     passed = swapped(lax.dynamic_index_in_dim(gradients, 1 - core, 0, keepdims=False))
     kept = lax.dynamic_index_in_dim(gradients, core, 0, keepdims=False)
     first = core == 0
-    batches = [jnp.where(first, kept, passed), jnp.where(first, passed, kept)]
-    slots = 2 * NX * NY * NZ
-    placed = [
-        jnp.zeros((slots, 2, PR, PW), F32)
-        .at[cell_slot[batch]]
-        .set(batches[batch])
-        .reshape(slots // 2, 2, 2, PR, PW)
-        for batch in range(MB)
-    ]
+    batches = jnp.stack([jnp.where(first, kept, passed), jnp.where(first, passed, kept)])
+    owners = NX * NY * NZ
+    placed = (
+        jnp.zeros((owners * MB * 2, 2, PR, PW), F32)
+        .at[place_in_all(cell_slot)]
+        .set(batches.reshape(-1, 2, PR, PW))
+    )
     returned = lax.all_to_all(
-        jnp.stack(placed, axis=1), "tile", split_axis=0, concat_axis=0, tiled=True
+        placed.reshape(owners, MB, 2, 2, PR, PW), "tile", split_axis=0, concat_axis=0, tiled=True
     )
     outbound = jnp.swapaxes(send_plan, 0, 1)
     target = jnp.where(outbound < 0, OWN, outbound).reshape(-1)
@@ -995,26 +1037,25 @@
 def body(dft, move, object_slices, probe_wave, intensities, send_list, cell_slot):
     owned = object_slices[0]
     send_plan = send_list[0]
-    wanted = jnp.transpose(send_plan.reshape(MB, NY, NZ, NX, 2), (2, 1, 3, 0, 4))
-    wanted = jnp.pad(wanted.reshape(NZ, 1, 64), ((0, 0), (0, 0), (0, 64)))
-    wanted = jnp.broadcast_to(wanted, (NZ, 8, 128))
-    windows, table, flag = fetch_windows(
-        owned.reshape(OWN, CHUNKS, TALL, PW), wanted, cell_slot.reshape(1, MB * CELLS)
-    )
-    crowded = flag[0, 0] > 0
-    windows = lax.cond(
-        crowded,
-        lambda: full_windows(owned, send_plan, cell_slot),
-        lambda: windows,
-    )
-    gradients = position_gradients(windows, probe_wave, intensities, dft, move)
-    sums = lax.cond(
-        crowded,
-        lambda: full_sums(gradients, send_plan, cell_slot),
-        lambda: return_gradients(
-            gradients.reshape(2, CELLS, CHUNKS, TALL, PW), table
-        ).reshape(OWN, 2, PR, PW),
-    )
+    meta = jnp.transpose(send_plan, (0, 2, 1)).reshape(MB * 2, NX * NY * NZ)
+    meta = lax.optimization_barrier(meta)
+    sums, flag = object_sums(
+        owned.reshape(OWN, CHUNKS, TALL, PW),
+        meta,
+        cell_slot,
+        probe_wave,
+        intensities,
+        dft,
+        move,
+    )
+
+    def full():
+        plan = jnp.transpose(meta.reshape(MB, 2, NX * NY * NZ), (0, 2, 1))
+        windows = full_windows(owned, plan, cell_slot)
+        gradients = position_gradients(windows, probe_wave, intensities, dft, move)
+        return full_sums(gradients.reshape(2, CELLS, 2, PR, PW), plan, cell_slot)
+
+    sums = lax.cond(flag[0, 0] > 0, full, lambda: sums.reshape(OWN, 2, PR, PW))
     return sums[None]
 
 

time: 151 us -> 143 us (0.947)
  local copies, waits for them, and re-layouts: 5.78 us -> 0.8 us
  Pallas kernels: 144 us -> 142 us
    pallas_call x3 -> x1, Pallas kernels: 144 us -> 142 us  [object_sums(): pl.pallas_call(whole_kernel, out_shape=(jax.ShapeDtypeStruct((OWN * CHUNK...]
where the time goes in v4:
time: 143 us
  Pallas kernels  142 us (99%)
    pallas_call x1, Pallas kernels, object_sums(): pl.pallas_call(whole_kernel, out_shape=(jax.ShapeDtypeStruct((OWN * CHUNK...  142 us

profile of v4, /device:TPU:32, one launch (start us, length us, event | category | flops | bytes accessed | tf_op | source)
XLA Modules:
  0.0 143.4 jit_solution(6476031406225303726)
XLA Ops:
  0.0 141.7 %object_sums.1 = (f32[1024,128]{1,0:T(8,128)S(1)}, s32[1,1]{1,0:T(1,128)}) custom-call(f32[32,8,4,128]{3,2,1,0:T(4,128)} %bitcast.51, s32[4,128]{1,0:T(4,128)} %bitcast.60, s32[2,32]{1,0:T(2,128)} %cells.1, f32[2,256,256]{2,1,0:T(8,128)} %probe.1, f32[2,256,256]{2,1,0:T(8,128)} %measured.1, bf16[512,512]{1,0:T(8,128)(2,1)} %constant.47.clone.dft, ...), custom_call_target="tpu_custom_call" | custom-call | tf_op jit(solution)/shard_map/object_sums/pallas_call | solution.py:975
  142.3 0.2 conditional.1
  142.6 0.8 copy.19

commit v5 on v4

--- a/solution.py
+++ b/solution.py
@@ -36,142 +36,142 @@
     ("s", 1, 1, 1),
     ("s", 2, -1, 1),
     ("s", 2, 1, 1),
+    ("s", 3, -1, 1),
+    ("s", 3, 1, 1),
+    ("s", 4, -1, 1),
+    ("s", 4, 1, 1),
     ("s", 0, -1, 2),
     ("s", 0, 1, 2),
     ("s", 1, -1, 2),
     ("s", 1, 1, 2),
     ("s", 2, -1, 2),
     ("s", 2, 1, 2),
+    ("s", 3, -1, 2),
+    ("s", 3, 1, 2),
+    ("s", 4, -1, 2),
+    ("s", 4, 1, 2),
     ("s", 0, -1, 3),
     ("s", 0, 1, 3),
     ("s", 1, -1, 3),
     ("s", 1, 1, 3),
     ("s", 2, -1, 3),
     ("s", 2, 1, 3),
+    ("s", 3, -1, 3),
+    ("s", 3, 1, 3),
+    ("s", 4, -1, 3),
+    ("s", 4, 1, 3),
     ("s", 0, 1, 4),
-    ("s", 3, -1, 1),
+    ("s", 5, -1, 1),
     ("s", 1, -1, 4),
-    ("s", 3, 1, 1),
+    ("s", 5, 1, 1),
     ("s", 2, 1, 4),
-    ("s", 4, -1, 1),
-    ("s", 3, -1, 2),
-    ("x", 0),
-    ("s", 4, 1, 1),
-    ("x", 1),
-    ("s", 3, 1, 2),
-    ("s", 5, -1, 1),
-    ("s", 4, -1, 2),
-    ("x", 2),
-    ("s", 5, 1, 1),
-    ("s", 3, -1, 3),
-    ("s", 4, 1, 2),
-    ("s", 5, -1, 2),
-    ("s", 3, 1, 3),
-    ("y", 0),
-    ("s", 4, -1, 3),
-    ("s", 5, 1, 2),
+    ("s", 6, -1, 1),
     ("s", 3, -1, 4),
-    ("s", 4, 1, 3),
-    ("y", 1),
-    ("s", 5, -1, 3),
     ("s", 6, 1, 1),
-    ("s", 5, 1, 3),
-    ("y", 2),
-    ("s", 6, -1, 1),
-    ("x", 3),
     ("s", 4, 1, 4),
     ("s", 7, -1, 1),
-    ("s", 5, -1, 4),
+    ("s", 5, -1, 2),
+    ("x", 0),
+    ("s", 7, 1, 1),
+    ("x", 1),
+    ("s", 5, 1, 2),
+    ("s", 6, -1, 2),
+    ("x", 2),
+    ("x", 3),
     ("s", 6, 1, 2),
-    ("t", 0),
-    ("s", 6, -1, 2),
-    ("s", 7, 1, 1),
+    ("s", 7, -1, 2),
     ("x", 4),
-    ("s", 7, -1, 2),
-    ("y", 3),
-    ("s", 6, 1, 3),
-    ("x", 5),
+    ("y", 0),
+    ("s", 5, -1, 3),
     ("s", 7, 1, 2),
     ("s", 6, -1, 3),
+    ("s", 5, 1, 3),
+    ("y", 1),
+    ("s", 6, 1, 3),
     ("s", 7, -1, 3),
+    ("s", 5, -1, 4),
+    ("s", 7, 1, 3),
+    ("y", 2),
     ("s", 6, 1, 4),
+    ("s", 7, -1, 4),
+    ("y", 3),
+    ("t", 0),
+    ("x", 5),
     ("y", 4),
-    ("s", 7, 1, 3),
-    ("t", 1),
-    ("s", 7, -1, 4),
-    ("y", 5),
     ("x", 6),
     ("x", 7),
-    ("t", 2),
+    ("t", 1),
+    ("y", 5),
     ("y", 6),
     ("y", 7),
+    ("t", 2),
     ("t", 3),
 )
 RETURN = (
     ("x", 0),
     ("x", 1),
+    ("x", 2),
     ("a", 0),
-    ("x", 2),
+    ("x", 3),
     ("a", 1),
-    ("x", 3),
+    ("x", 4),
     ("p", 0, -1, 2),
     ("p", 0, 1, 2),
-    ("x", 4),
     ("a", 2),
+    ("x", 5),
     ("p", 1, -1, 2),
     ("p", 1, 1, 2),
+    ("a", 3),
     ("p", 0, -1, 3),
     ("p", 0, 1, 3),
-    ("x", 5),
-    ("a", 3),
+    ("x", 6),
+    ("a", 4),
     ("p", 2, -1, 2),
     ("p", 2, 1, 2),
-    ("x", 6),
-    ("a", 4),
     ("p", 1, -1, 3),
     ("p", 1, 1, 3),
-    ("p", 0, 1, 4),
     ("x", 7),
+    ("a", 5),
     ("p", 3, -1, 2),
     ("p", 3, 1, 2),
-    ("a", 5),
-    ("p", 2, -1, 3),
-    ("p", 2, 1, 3),
+    ("p", 0, 1, 4),
     ("p", 4, -1, 2),
     ("p", 4, 1, 2),
     ("a", 6),
+    ("p", 2, -1, 3),
+    ("p", 2, 1, 3),
     ("p", 1, -1, 4),
-    ("p", 3, -1, 3),
-    ("f", 0),
     ("a", 7),
-    ("p", 3, 1, 3),
     ("p", 5, -1, 2),
     ("p", 5, 1, 2),
-    ("p", 2, 1, 4),
+    ("p", 3, -1, 3),
+    ("p", 3, 1, 3),
     ("p", 4, -1, 3),
+    ("f", 0),
+    ("p", 6, -1, 2),
     ("p", 4, 1, 3),
-    ("p", 6, -1, 2),
     ("p", 6, 1, 2),
     ("f", 1),
-    ("p", 3, -1, 4),
+    ("p", 2, 1, 4),
+    ("p", 7, -1, 2),
     ("p", 7, 1, 2),
-    ("p", 7, -1, 2),
     ("p", 5, -1, 3),
     ("p", 5, 1, 3),
-    ("f", 2),
+    ("p", 3, -1, 4),
     ("p", 4, 1, 4),
     ("p", 6, -1, 3),
     ("p", 6, 1, 3),
+    ("p", 7, -1, 3),
+    ("f", 2),
+    ("p", 5, -1, 4),
+    ("p", 7, 1, 3),
     ("f", 3),
-    ("p", 7, -1, 3),
-    ("p", 7, 1, 3),
-    ("p", 5, -1, 4),
     ("f", 4),
+    ("p", 7, -1, 4),
     ("p", 6, 1, 4),
-    ("p", 7, -1, 4),
     ("f", 5),
+    ("f", 7),
     ("f", 6),
-    ("f", 7),
 )
 
 
@@ -427,7 +427,7 @@
     ]
     picks = jnp.dot(jnp.concatenate(picks, axis=0), column, preferred_element_type=F32)
     for part in range(PLACES // 8):
-        tables[1 + part] = picks[part * 8 : part * 8 + 8].astype(I32)
+        tables[1 + part] = picks[part * 8 : part * 8 + 8].astype(I32) - 1
         table_copy(1 + part, pick.at[part]).start()
     over_x = jnp.where(jnp.max(whole, axis=1, keepdims=True) > PLACES, 1.0, 0.0)
     over_z = jnp.max(
@@ -492,7 +492,7 @@
         def fill(part, carry):
             for k in range(8):
                 for to in range(NX):
-                    index = jnp.clip(pick[part, k, z * 4 + to], 1, COLUMN) - 1
+                    index = pick[part, k, z * 4 + to] & (COLUMN - 1)
                     x_pack[chunk, to * PLACES + part * 8 + k] = ag[chunk][index]
             return carry
 
@@ -509,7 +509,7 @@
         def fill(part, carry):
             for k in range(8):
                 for to in range(NY):
-                    index = jnp.clip(turn[to, part * 8 + k], 1, ROWS) - 1
+                    index = turn[to, part * 8 + k] & (ROWS - 1)
                     y_pack[chunk, to * PLACES + part * 8 + k] = x_recv[chunk][index]
             return carry
 
@@ -536,7 +536,7 @@
         part, half = quarter // 2, quarter % 2
 
         def both(index):
-            index = jnp.clip(index, 0, ROWS - 1)
+            index = index & (ROWS - 1)
             return jnp.concatenate([y_recv[low][index], y_recv[high][index]], axis=0)
 
         def lay(r, carry):
@@ -582,13 +582,13 @@
         inside = (wide >= first) & (wide < first + many)
         onward.append(
             jnp.sum(
-                jnp.where(inside, giver * PLACES + low + wide - first + 1.0, 0.0),
+                jnp.where(inside, giver * PLACES + low + wide - first, 0.0),
                 axis=0,
                 keepdims=True,
             )
         )
         inside = (wide >= low) & (wide < low + many)
-        back = back + jnp.where(inside, to * PLACES + first + wide - low + 1.0, 0.0)
+        back = back + jnp.where(inside, to * PLACES + first + wide - low, 0.0)
     tables[last] = jnp.concatenate(onward + [jnp.zeros((4, 128), F32)], axis=0).astype(I32)
     table_copy(last, turn).start()
     tab[8:12, :] = back.astype(I32)
@@ -779,7 +779,7 @@
         pair_copy(chunk).wait_recv()
 
         def fill_y(row):
-            index = jnp.clip(places[0, row], 0, MB * CELLS - 1)
+            index = places[0, row] & (MB * CELLS - 1)
             y_pack[chunk, row] = cells[chunk][index]
 
         fill_rows(ROWS, fill_y)
@@ -794,7 +794,7 @@
 
         def fill_x(pair):
             to, k = pair // (PLACES // 2), pair % (PLACES // 2) * 2
-            two = [jnp.clip(places[8 + to, k + i], 1, ROWS) - 1 for i in range(2)]
+            two = [places[8 + to, k + i] & (ROWS - 1) for i in range(2)]
             spot = pl.ds(pl.multiple_of(pair * 2 * TALL, 8), 2 * TALL)
             x_pack[chunk, spot] = jnp.concatenate([y_recv[chunk][i] for i in two], axis=0)
 

time: 143 us -> 142 us (level); the launches traced: 143 us -> 140 us
  Pallas kernels: 142 us -> 139 us
    pallas_call x1, Pallas kernels: 142 us -> 139 us  [object_sums(): pl.pallas_call(whole_kernel, out_shape=(jax.ShapeDtypeStruct((OWN * CHUNK...]
where the time goes in v5:
time: 142 us; the launch traced here: 140 us
  Pallas kernels  139 us (98%)
    pallas_call x1, Pallas kernels, object_sums(): pl.pallas_call(whole_kernel, out_shape=(jax.ShapeDtypeStruct((OWN * CHUNK...  139 us

profile of v5, /device:TPU:32, one launch (start us, length us, event | category | flops | bytes accessed | tf_op | source)
XLA Modules:
  0.0 140.5 jit_solution(2247774159104548857)
XLA Ops:
  0.0 138.8 %object_sums.1 = (f32[1024,128]{1,0:T(8,128)S(1)}, s32[1,1]{1,0:T(1,128)}) custom-call(f32[32,8,4,128]{3,2,1,0:T(4,128)} %bitcast.51, s32[4,128]{1,0:T(4,128)} %bitcast.60, s32[2,32]{1,0:T(2,128)} %cells.1, f32[2,256,256]{2,1,0:T(8,128)} %probe.1, f32[2,256,256]{2,1,0:T(8,128)} %measured.1, bf16[512,512]{1,0:T(8,128)(2,1)} %constant.47.clone.dft, ...), custom_call_target="tpu_custom_call" | custom-call | tf_op jit(solution)/shard_map/object_sums/pallas_call | solution.py:975
  139.4 0.2 conditional.1
  139.7 0.8 copy.19

commit v6 on v5

--- a/solution.py
+++ b/solution.py
@@ -519,12 +519,12 @@
         own = pl.ds(y * PLACES, PLACES)
         y_recv[chunk][own] = y_pack[chunk, own]
 
-    def pair_copy(part):
+    def pair_copy(quarter):
         return send_to(
-            other.at[part],
-            win.at[core, part],
-            pair_send.at[part],
-            pair_recv.at[part],
+            other.at[quarter // 2, quarter % 2],
+            win.at[core, quarter // 2, quarter % 2],
+            pair_send.at[quarter],
+            pair_recv.at[quarter],
             partner,
         )
 
@@ -540,12 +540,12 @@
             return jnp.concatenate([y_recv[low][index], y_recv[high][index]], axis=0)
 
         def lay(r, carry):
-            first = pl.multiple_of(r * PR + half * 8, 8)
+            first = pl.multiple_of(r * 8, 8)
             for side in range(2):
                 k = r * 2 + side
                 lanes_of = slice(side * PW, side * PW + PW)
-                win[core, part, pl.ds(first, 8), lanes_of] = both(slot[0, core * CELLS + k])
-                other[part, pl.ds(first, 8), lanes_of] = both(slot[0, (1 - core) * CELLS + k])
+                win[core, part, half, pl.ds(first, 8), lanes_of] = both(slot[0, core * CELLS + k])
+                other[part, half, pl.ds(first, 8), lanes_of] = both(slot[0, (1 - core) * CELLS + k])
             return carry
 
         lax.fori_loop(0, W // PR, lay, 0)
@@ -560,8 +560,7 @@
                 along_y(event[1])
             else:
                 take(event[1])
-                if event[1] % 2 == 1:
-                    pair_copy(event[1] // 2).start()
+                pair_copy(event[1]).start()
 
     run(FETCH[first_x:first_y])
 
@@ -626,8 +625,8 @@
             y_copy(chunk, step).wait_send()
     crowded.wait()
     flag[0, 0] = turned[0, 0]
-    pair_copy(0).wait()
-    pair_copy(1).wait()
+    for quarter in range(4):
+        pair_copy(quarter).wait()
 
 
 def parts(value):
@@ -657,18 +656,34 @@
     return from_right(real, imag, table, sign)
 
 
+def window(win, index):
+    if len(win.shape) == 4:
+        return win[index, 0], win[index, 1]
+    return tuple(
+        jnp.concatenate(
+            [
+                win[index, part, half, r * 8 : r * 8 + 8]
+                for r in range(W // PR)
+                for half in range(2)
+            ],
+            axis=0,
+        )
+        for part in range(2)
+    )
+
+
 def position(win, probe, measured, dft, move, lay):
     pr, pi = probe[0], probe[1]
-    ar, ai = win[0, 0], win[0, 1]
+    ar, ai = window(win, 0)
     wave_r, wave_i = both_sides(pr * ar - pi * ai, pr * ai + pi * ar, move, 1.0)
-    br, bi = win[1, 0], win[1, 1]
+    br, bi = window(win, 1)
     far_r, far_i = both_sides(
         wave_r * br - wave_i * bi, wave_r * bi + wave_i * br, dft, 1.0
     )
     gap = far_r * far_r + far_i * far_i - measured[...]
     back_r, back_i = both_sides(gap * far_r, gap * far_i, dft, -1.0)
     lay(1, wave_r * back_r + wave_i * back_i, wave_r * back_i - wave_i * back_r)
-    br, bi = win[1, 0], win[1, 1]
+    br, bi = window(win, 1)
     low_r, low_i = both_sides(
         br * back_r + bi * back_i, br * back_i - bi * back_r, move, -1.0
     )
@@ -912,7 +927,7 @@
     dma = pltpu.SemaphoreType.DMA
     many, one = pltpu.VMEM((CHUNKS, ROWS) + strip, F32), pltpu.VMEM((ROWS,) + strip, F32)
     fetching = dict(
-        win=pltpu.VMEM((2, 2, W, W), F32),
+        win=pltpu.VMEM((2, 2, 2, W // 2, W), F32),
         tab=pltpu.VMEM((16, 128), I32),
         ag=[pltpu.VMEM((COLUMN,) + strip, F32)] * CHUNKS,
         metas=pltpu.VMEM(tile, I32),
@@ -931,7 +946,7 @@
         marks_x=pltpu.VMEM((NX,) + tile, I32),
         marks_y=pltpu.VMEM((NY,) + tile, I32),
         marks_z=pltpu.VMEM((NZ,) + tile, I32),
-        other=pltpu.VMEM((2, W, W), F32),
+        other=pltpu.VMEM((2, 2, W // 2, W), F32),
         ag_send=dma((CHUNKS, 2, 4)),
         ag_recv=dma((CHUNKS, 2, 4)),
         meta_send=dma((NZ,)),
@@ -942,8 +957,8 @@
         x_sem=dma((CHUNKS, NX)),
         y_send=dma((CHUNKS, NY)),
         y_sem=dma((CHUNKS, NY)),
-        pair_send=dma((2,)),
-        pair_recv=dma((2,)),
+        pair_send=dma((4,)),
+        pair_recv=dma((4,)),
         local_sem=dma((3 + PLACES // 8,)),
     )
     giving = dict(

time: 142 us -> 141 us (level)
  no operation moved by 1% of the time
where the time goes in v6:
time: 141 us; the launch traced here: 140 us
  Pallas kernels  139 us (99%)
    pallas_call x1, Pallas kernels, object_sums(): pl.pallas_call(whole_kernel, out_shape=(jax.ShapeDtypeStruct((OWN * CHUNK...  139 us

profile of v6, /device:TPU:32, one launch (start us, length us, event | category | flops | bytes accessed | tf_op | source)
XLA Modules:
  0.0 140.3 jit_solution(2170219522514306257)
XLA Ops:
  0.0 138.7 %object_sums.1 = (f32[1024,128]{1,0:T(8,128)S(1)}, s32[1,1]{1,0:T(1,128)}) custom-call(f32[32,8,4,128]{3,2,1,0:T(4,128)} %bitcast.51, s32[4,128]{1,0:T(4,128)} %bitcast.60, s32[2,32]{1,0:T(2,128)} %cells.1, f32[2,256,256]{2,1,0:T(8,128)} %probe.1, f32[2,256,256]{2,1,0:T(8,128)} %measured.1, bf16[512,512]{1,0:T(8,128)(2,1)} %constant.47.clone.dft, ...), custom_call_target="tpu_custom_call" | custom-call | tf_op jit(solution)/shard_map/object_sums/pallas_call | solution.py:990
  139.3 0.2 conditional.1
  139.5 0.8 copy.19

commit v7 on v6

--- a/solution.py
+++ b/solution.py
@@ -292,6 +292,7 @@
     pair_recv,
     local_sem,
     loads,
+    mix,
 ):
     core, y, z, x = place()
     partner = device(1 - core, y, z, x)
@@ -623,6 +624,9 @@
         for step in range(1, NX):
             x_copy(chunk, step).wait_send()
             y_copy(chunk, step).wait_send()
+    mix[...] = jnp.where(
+        jnp.broadcast_to(tab[1:2, :], (COLUMN, ROWS)) == iota((COLUMN, ROWS), 0) + 1, 1.0, 0.0
+    ).astype(BF16)
     crowded.wait()
     flag[0, 0] = turned[0, 0]
     for quarter in range(4):
@@ -765,12 +769,7 @@
 
     for chunk in range(CHUNKS):
         cells[chunk][pl.ds(core * CELLS, CELLS)] = grad[core, :, chunk]
-    for chunk in range(CHUNKS):
         pair_copy(chunk).start()
-
-    mix[...] = jnp.where(
-        jnp.broadcast_to(tab[1:2, :], (COLUMN, ROWS)) == iota((COLUMN, ROWS), 0) + 1, 1.0, 0.0
-    ).astype(BF16)
 
     def y_copy(chunk, step):
         return send_to(
@@ -912,7 +911,7 @@
             )
         )
     ]
-    fetch(obj, meta, cells, flag=flag, loads=loads, **fetching)
+    fetch(obj, meta, cells, flag=flag, loads=loads, mix=giving["mix"], **fetching)
     for load in loads:
         load.wait()
     position(win, probe_in, measured_in, dft_in, move_in, lay_cells(grad))

time: 141 us -> 141 us (level)
  no operation moved by 1% of the time
where the time goes in v7:
time: 141 us; the launch traced here: 140 us
  Pallas kernels  139 us (99%)
    pallas_call x1, Pallas kernels, object_sums(): pl.pallas_call(whole_kernel, out_shape=(jax.ShapeDtypeStruct((OWN * CHUNK...  139 us

profile of v7, /device:TPU:32, one launch (start us, length us, event | category | flops | bytes accessed | tf_op | source)
XLA Modules:
  0.0 140.2 jit_solution(4589685245659002348)
XLA Ops:
  0.0 138.5 %object_sums.1 = (f32[1024,128]{1,0:T(8,128)S(1)}, s32[1,1]{1,0:T(1,128)}) custom-call(f32[32,8,4,128]{3,2,1,0:T(4,128)} %bitcast.51, s32[4,128]{1,0:T(4,128)} %bitcast.60, s32[2,32]{1,0:T(2,128)} %cells.1, f32[2,256,256]{2,1,0:T(8,128)} %probe.1, f32[2,256,256]{2,1,0:T(8,128)} %measured.1, bf16[512,512]{1,0:T(8,128)(2,1)} %constant.47.clone.dft, ...), custom_call_target="tpu_custom_call" | custom-call | tf_op jit(solution)/shard_map/object_sums/pallas_call | solution.py:989
  139.2 0.2 conditional.1
  139.4 0.8 copy.19
